TPU v7x, 8 devices: a whole 2x2x1 slice. The times are simulated.
8 devices in a mesh: replica: 2 (over z, y), dp: 4 (over x, core).
Axes of the slice: x: 2, y: 2, z: 1, core: 2. Of those that a mesh axis runs over, the one named last changes fastest.
Arguments:
- x: bfloat16 [1024, 256], P(('replica', 'dp')), parts along dimension 0
- lengths: int32 [1024], P(('replica', 'dp')), parts along dimension 0
- cache: bfloat16 [2, 1024, 512, 576], P(None, ('replica', 'dp')), parts along dimension 1
- w_q: bfloat16 [2, 256, 1152], replicated
- w_o: bfloat16 [2, 1024, 256], replicated
- expert_ids: int32 [2, 1024, 6], P(None, ('replica', 'dp')), parts along dimension 1
- slots: int32 [2, 1024, 6], P(None, ('replica', 'dp')), parts along dimension 1
- route_w: float32 [2, 1024, 6], P(None, ('replica', 'dp')), parts along dimension 1
- w1_exp: bfloat16 [2, 64, 256, 176], P(None, 'dp')
- w3_exp: bfloat16 [2, 64, 256, 176], P(None, 'dp')
- w2_exp: bfloat16 [2, 64, 176, 256], P(None, 'dp')
- w1_sh: bfloat16 [2, 256, 352], P(None, None, 'dp')
- w3_sh: bfloat16 [2, 256, 352], P(None, None, 'dp')
- w2_sh: bfloat16 [2, 352, 256], P(None, 'dp')
Outputs:
- output: bfloat16 [1024, 256], P(('replica', 'dp')), parts along dimension 0
There are 2 independent parts. A program takes and returns all parts, laid end to end along the dimension named above; an argument that names none is the same for every part.
All inputs are finite; a program needn't handle non-finite values.
Results may differ from a plain program's by a relative error of at most 0.02.
Values are sent between devices in bfloat16 or wider.
A program may use at most 1 GiB of HBM per device.

v0:
```python
import jax
import jax.numpy as jnp
from jax import lax
from jax.sharding import PartitionSpec as P

NORM_EPS = 1e-6
ATT_SCALE = 1.0 / (192.0 ** 0.5)
LATENT = 512


def rms_norm(values):
    vals32 = values.astype(jnp.float32)
    return vals32 * lax.rsqrt(jnp.mean(vals32 * vals32, axis=-1, keepdims=True) + NORM_EPS)


def gated_hidden(tok_in, w_up, w_gate):
    gate_in = jnp.dot(tok_in, w_gate, preferred_element_type=jnp.float32)
    up_in = jnp.dot(tok_in, w_up, preferred_element_type=jnp.float32)
    return (jax.nn.silu(gate_in) * up_in).astype(jnp.bfloat16)


def local_attention(resid, lengths, cache_l, w_q_l, w_o_l):
    tok_count = resid.shape[0]
    seq_len, kv_dim = cache_l.shape[1], cache_l.shape[2]
    num_heads = w_q_l.shape[1] // kv_dim
    normed = rms_norm(resid).astype(jnp.bfloat16)
    queries = jnp.dot(normed, w_q_l, preferred_element_type=jnp.float32).astype(jnp.bfloat16)
    queries = queries.reshape(tok_count, num_heads, kv_dim)
    scores = jnp.einsum('bhc,btc->bht', queries, cache_l, preferred_element_type=jnp.float32) * ATT_SCALE
    valid = jnp.arange(seq_len)[None, None, :] < lengths[:, None, None]
    probs = jax.nn.softmax(jnp.where(valid, scores, -jnp.inf), axis=-1).astype(jnp.bfloat16)
    attn = jnp.einsum('bht,btc->bhc', probs, cache_l[:, :, :LATENT], preferred_element_type=jnp.float32)
    attn = attn.astype(jnp.bfloat16).reshape(tok_count, num_heads * LATENT)
    return (resid.astype(jnp.float32) + jnp.dot(attn, w_o_l, preferred_element_type=jnp.float32)).astype(jnp.bfloat16)


def route_select(ids_l, slot_l, experts, capacity):
    buf_rows = jnp.where(slot_l >= 0, ids_l * capacity + slot_l, -1)
    return (buf_rows[:, :, None] == jnp.arange(experts * capacity)).astype(jnp.bfloat16)


def solution(mesh):
    group = mesh.shape['dp']
    tok_axes = ('replica', 'dp')
    in_specs = (
        P(tok_axes, None), P(tok_axes), P(None, tok_axes, None, None),
        P(None, None, None), P(None, None, None),
        P(None, tok_axes, None), P(None, tok_axes, None), P(None, tok_axes, None),
        P(None, 'dp', None, None), P(None, 'dp', None, None), P(None, 'dp', None, None),
        P(None, None, 'dp'), P(None, None, 'dp'), P(None, 'dp', None),
    )

    def device_step(x, lengths, cache, w_q, w_o, expert_ids, slots, route_w, w1_exp, w3_exp, w2_exp, w1_sh, w3_sh, w2_sh):
        batch_dev, d_model = x.shape
        local_experts = w1_exp.shape[1]
        experts = local_experts * group
        top_k = expert_ids.shape[2]
        capacity = max(1, (2 * batch_dev * top_k) // experts)
        resid = x
        for layer_idx in range(cache.shape[0]):
            resid = local_attention(resid, lengths, cache[layer_idx], w_q[layer_idx], w_o[layer_idx])
            ffn_in = rms_norm(resid).astype(jnp.bfloat16)
            gathered = lax.all_gather(ffn_in, 'dp', axis=0, tiled=True)
            shared_h = gated_hidden(gathered, w1_sh[layer_idx], w3_sh[layer_idx])
            shared_part = jnp.dot(shared_h, w2_sh[layer_idx], preferred_element_type=jnp.float32)
            shared_out = lax.psum_scatter(shared_part, 'dp', scatter_dimension=0, tiled=True)
            select = route_select(expert_ids[layer_idx], slots[layer_idx], experts, capacity)
            dispatch = jnp.sum(select, axis=1)
            send_buf = jnp.einsum('br,bd->rd', dispatch, ffn_in, preferred_element_type=jnp.float32).astype(jnp.bfloat16)
            send_buf = send_buf.reshape(group, local_experts, capacity, d_model)
            recv_buf = lax.all_to_all(send_buf, 'dp', 0, 0, tiled=True)
            gate_in = jnp.einsum('sncd,ndf->nscf', recv_buf, w3_exp[layer_idx], preferred_element_type=jnp.float32)
            up_in = jnp.einsum('sncd,ndf->nscf', recv_buf, w1_exp[layer_idx], preferred_element_type=jnp.float32)
            hidden = (jax.nn.silu(gate_in) * up_in).astype(jnp.bfloat16)
            expert_out = jnp.einsum('nscf,nfd->sncd', hidden, w2_exp[layer_idx], preferred_element_type=jnp.float32).astype(jnp.bfloat16)
            returned = lax.all_to_all(expert_out, 'dp', 0, 0, tiled=True)
            returned = returned.reshape(experts * capacity, d_model)
            picked = jnp.einsum('cls,se->cle', select, returned, preferred_element_type=jnp.float32)
            routed = jnp.sum(route_w[layer_idx][:, :, None] * picked, axis=1)
            resid = (resid.astype(jnp.float32) + routed + shared_out).astype(jnp.bfloat16)
        return resid

    return jax.shard_map(device_step, mesh=mesh, in_specs=in_specs, out_specs=P(tok_axes, None), check_vma=False)
```

profile of v0, /device:TPU:0, one launch (start us, length us, event | category | flops | bytes accessed | tf_op | source)
XLA Modules:
  0.0 315.5 jit_solution(4371123875087118116)
XLA Ops:
  6.5 0.8 iota_compare_fusion.12
  7.3 0.9 fusion.98
  8.3 1.4 convolution_convert_fusion.3
  9.9 0.8 copy.36
  10.7 97.0 %slice_bitcast_fusion.1 = (bf16[128,512,576]{1,2,0:T(8,128)(2,1)}, bf16[128,512,576]{1,2,0:T(8,128)(2,1)}) fusion(bf16[2,128,512,576]{2,3,1,0:T(8,128)(2,1)} %param.16), kind=kLoop, calls=%fused_computation.3 | loop fusion | bytes 301989888 | tf_op jit(solution)/shard_map/squeeze | solution.py:61
  107.7 25.3 %fusion.50 = f32[128,2,512]{2,1,0:T(2,128)S(1)} fusion(bf16[128,2,576]{2,1,0:T(2,128)(2,1)S(1)} %copy.36, pred[128,512]{1,0:T(8,128)(4,1)S(1)} %iota_compare_fusion.12, bf16[2,128,512,576]{2,3,1,0:T(8,128)(2,1)} %param.16), kind=kOutput, calls=%fused_computation.54 | convolution fusion | flops 151257088 | bytes 76382208 | tf_op jit(solution)/shard_map/bhc,btc->bht/dot_general | solution.py:29
  133.7 25.6 %fusion.52 = bf16[128,2,512]{2,1,0:T(2,128)(2,1)S(1)} fusion(bf16[128,512,576]{1,2,0:T(8,128)(2,1)} %get-tuple-element.7, f32[128,2,512]{2,1,0:T(2,128)S(1)} %get-tuple-element.16, f32[128,2]{1,0:T(8,128)S(1)} %get-tuple-element.15), kind=kOutput, calls=%fused_computation.56 | convolution fusion | flops 134610944 | bytes 67896320 | tf_op jit(solution)/shard_map/bht,btc->bhc/dot_general | solution.py:32
  160.6 1.3 convolution_convert_fusion.1
  161.9 4.6 %all-to-all-start = ((bf16[4,16,24,256]{3,2,1,0:T(8,128)(2,1)}), bf16[4,16,24,256]{3,2,1,0:T(8,128)(2,1)S(1)}, u32[]{:S(2)}, u32[]{:S(2)}) async-start(bf16[4,16,24,256]{3,2,1,0:T(8,128)(2,1)} %bitcast.6), calls=%async_computation | async-start | bytes 1572864 | tf_op jit(solution)/shard_map/all_to_all | solution.py:71
  166.5 14.8 %all_gather.6 = bf16[512,256]{1,0:T(8,128)(2,1)S(1)} all-gather(bf16[128,256]{1,0:T(8,128)(2,1)S(1)} %multiply_convert_fusion.3), channel_id=1, replica_groups=mesh['replica'=2,'dp'=4] {'dp'}, dimensions={0}, use_global_device_ids=true | all-gather | bytes 327680 | tf_op jit(solution)/shard_map/all_gather | solution.py:63
  181.5 1.3 fusion.65
  182.9 2.0 fusion.22
  184.8 2.8 fusion.41
  187.6 1.0 copy.43
  188.6 3.7 %all-to-all-start.1 = ((bf16[4,16,24,256]{3,2,1,0:T(8,128)(2,1)}), bf16[4,16,24,256]{3,2,1,0:T(8,128)(2,1)S(1)}, u32[]{:S(2)}, u32[]{:S(2)}) async-start(bf16[4,16,24,256]{3,2,1,0:T(8,128)(2,1)} %copy.43), calls=%async_computation.1 | async-start | bytes 1572864 | tf_op jit(solution)/shard_map/all_to_all | solution.py:76
  193.0 13.2 %all-to-all-done.1 = bf16[4,16,24,256]{3,2,1,0:T(8,128)(2,1)S(1)} async-done(((bf16[4,16,24,256]{3,2,1,0:T(8,128)(2,1)}), bf16[4,16,24,256]{3,2,1,0:T(8,128)(2,1)S(1)}, u32[]{:S(2)}, u32[]{:S(2)}) %all-to-all-start.1) | async-done | bytes 786464 | tf_op jit(solution)/shard_map/all_to_all | solution.py:76
  206.3 1.0 fusion.49
  207.3 1.0 fusion.100
  208.9 0.8 copy.45
  209.6 25.3 %fusion.51 = f32[128,2,512]{2,1,0:T(2,128)S(1)} fusion(bf16[128,2,576]{2,1,0:T(2,128)(2,1)S(1)} %copy.45, pred[128,512]{1,0:T(8,128)(4,1)S(1)} %iota_compare_fusion.12, bf16[2,128,512,576]{2,3,1,0:T(8,128)(2,1)} %param.16), kind=kOutput, calls=%fused_computation.55 | convolution fusion | flops 151257088 | bytes 76382208 | tf_op jit(solution)/shard_map/bhc,btc->bht/dot_general | solution.py:29
  235.6 25.6 %fusion.55 = bf16[128,2,512]{2,1,0:T(2,128)(2,1)S(1)} fusion(bf16[128,512,576]{1,2,0:T(8,128)(2,1)} %get-tuple-element.8, f32[128,2,512]{2,1,0:T(2,128)S(1)} %get-tuple-element.20, f32[128,2]{1,0:T(8,128)S(1)} %get-tuple-element.19), kind=kOutput, calls=%fused_computation.57 | convolution fusion | flops 134610944 | bytes 67896320 | tf_op jit(solution)/shard_map/bht,btc->bhc/dot_general | solution.py:32
  261.7 1.3 convolution_convert_fusion
  263.0 3.5 %all-to-all-start.2 = ((bf16[4,16,24,256]{3,2,1,0:T(8,128)(2,1)}), bf16[4,16,24,256]{3,2,1,0:T(8,128)(2,1)S(1)}, u32[]{:S(2)}, u32[]{:S(2)}) async-start(bf16[4,16,24,256]{3,2,1,0:T(8,128)(2,1)} %bitcast.28), calls=%async_computation.3 | async-start | bytes 1572864 | tf_op jit(solution)/shard_map/all_to_all | solution.py:71
  266.5 14.7 %all_gather.7 = bf16[512,256]{1,0:T(8,128)(2,1)S(1)} all-gather(bf16[128,256]{1,0:T(8,128)(2,1)S(1)} %multiply_convert_fusion.2), channel_id=1, replica_groups=mesh['replica'=2,'dp'=4] {'dp'}, dimensions={0}, use_global_device_ids=true | all-gather | bytes 327680 | tf_op jit(solution)/shard_map/all_gather | solution.py:63
  281.4 1.3 fusion.64
  282.8 2.0 fusion.17
  284.8 2.7 fusion.38
  287.5 0.9 copy.52
  288.4 3.5 %all-to-all-start.3 = ((bf16[4,16,24,256]{3,2,1,0:T(8,128)(2,1)}), bf16[4,16,24,256]{3,2,1,0:T(8,128)(2,1)S(1)}, u32[]{:S(2)}, u32[]{:S(2)}) async-start(bf16[4,16,24,256]{3,2,1,0:T(8,128)(2,1)} %copy.52), calls=%async_computation.4 | async-start | bytes 1572864 | tf_op jit(solution)/shard_map/all_to_all | solution.py:76
  291.9 14.2 %all-to-all-done.3 = bf16[4,16,24,256]{3,2,1,0:T(8,128)(2,1)S(1)} async-done(((bf16[4,16,24,256]{3,2,1,0:T(8,128)(2,1)}), bf16[4,16,24,256]{3,2,1,0:T(8,128)(2,1)S(1)}, u32[]{:S(2)}, u32[]{:S(2)}) %all-to-all-start.3) | async-done | bytes 786464 | tf_op jit(solution)/shard_map/all_to_all | solution.py:76
  306.1 1.0 fusion.48
  307.1 1.6 add_convert_fusion
  (55 shorter events, 5.0 us)
Async XLA Ops:
  133.6 25.7 %copy-start.1 = (bf16[128,256]{1,0:T(8,128)(2,1)S(1)}, bf16[128,256]{1,0:T(8,128)(2,1)}, u32[]{:S(2)}) copy-start(bf16[128,256]{1,0:T(8,128)(2,1)} %param.14) | copy-start | bytes 196612
  133.6 25.7 %copy-start.6 = (bf16[2,1024,256]{2,1,0:T(8,128)(2,1)S(1)}, bf16[2,1024,256]{2,1,0:T(8,128)(2,1)}, u32[]{:S(2)}) copy-start(bf16[2,1024,256]{2,1,0:T(8,128)(2,1)} %param.18) | copy-start | bytes 3145732
  133.7 26.0 %copy-start.4 = (s32[2,128,6]{1,0,2:T(2,128)S(1)}, s32[2,128,6]{1,0,2:T(2,128)}, u32[]{:S(2)}) copy-start(s32[2,128,6]{1,0,2:T(2,128)} %param.19) | copy-start | bytes 18436
  133.7 26.0 %copy-start.5 = (s32[2,128,6]{1,0,2:T(2,128)S(1)}, s32[2,128,6]{1,0,2:T(2,128)}, u32[]{:S(2)}) copy-start(s32[2,128,6]{1,0,2:T(2,128)} %param.20) | copy-start | bytes 18436
  160.5 20.7 %copy-start.2 = (bf16[2,256,88]{1,2,0:T(8,128)(2,1)S(1)}, bf16[2,256,88]{1,2,0:T(8,128)(2,1)}, u32[]{:S(2)}) copy-start(bf16[2,256,88]{1,2,0:T(8,128)(2,1)} %param.26) | copy-start | bytes 270340
  160.6 20.9 %copy-start.8 = (bf16[2,88,256]{2,1,0:T(8,128)(2,1)S(1)}, bf16[2,88,256]{2,1,0:T(8,128)(2,1)}, u32[]{:S(2)}) copy-start(bf16[2,88,256]{2,1,0:T(8,128)(2,1)} %param.27) | copy-start | bytes 270340
  160.6 20.9 %copy-start.9 = (bf16[2,256,88]{1,2,0:T(8,128)(2,1)S(1)}, bf16[2,256,88]{1,2,0:T(8,128)(2,1)}, u32[]{:S(2)}) copy-start(bf16[2,256,88]{1,2,0:T(8,128)(2,1)} %param.25) | copy-start | bytes 270340
  161.9 21.0 %all-to-all-start = ((bf16[4,16,24,256]{3,2,1,0:T(8,128)(2,1)}), bf16[4,16,24,256]{3,2,1,0:T(8,128)(2,1)S(1)}, u32[]{:S(2)}, u32[]{:S(2)}) async-start(bf16[4,16,24,256]{3,2,1,0:T(8,128)(2,1)} %bitcast.6), calls=%async_computation | async-start | bytes 1572864 | tf_op jit(solution)/shard_map/all_to_all | solution.py:71
  166.5 40.8 %reduce-scatter.3.cloned.1.call-start = ((), (), s32[]{:S(2)}) async-start(), calls=%async_computation.6 | async-start | bytes 655360 | tf_op jit(solution)/shard_map/reduce_scatter | solution.py:66
  187.6 4.7 %copy-start.3 = (f32[2,128,6]{1,0,2:T(2,128)S(1)}, f32[2,128,6]{1,0,2:T(2,128)}, u32[]{:S(2)}) copy-start(f32[2,128,6]{1,0,2:T(2,128)} %param.21) | copy-start | bytes 18436
  188.6 17.7 %all-to-all-start.1 = ((bf16[4,16,24,256]{3,2,1,0:T(8,128)(2,1)}), bf16[4,16,24,256]{3,2,1,0:T(8,128)(2,1)S(1)}, u32[]{:S(2)}, u32[]{:S(2)}) async-start(bf16[4,16,24,256]{3,2,1,0:T(8,128)(2,1)} %copy.43), calls=%async_computation.1 | async-start | bytes 1572864 | tf_op jit(solution)/shard_map/all_to_all | solution.py:76
  206.3 2.0 copy-start
  235.6 25.7 %copy-start.7 = (bf16[2,1024,256]{2,1,0:T(8,128)(2,1)S(1)}, bf16[2,1024,256]{2,1,0:T(8,128)(2,1)}, u32[]{:S(2)}) copy-start(bf16[2,1024,256]{2,1,0:T(8,128)(2,1)} %param.18) | copy-start | bytes 3145732
  261.7 19.7 %copy-start.10 = (bf16[2,256,88]{1,2,0:T(8,128)(2,1)S(1)}, bf16[2,256,88]{1,2,0:T(8,128)(2,1)}, u32[]{:S(2)}) copy-start(bf16[2,256,88]{1,2,0:T(8,128)(2,1)} %param.25) | copy-start | bytes 270340
  263.0 19.8 %all-to-all-start.2 = ((bf16[4,16,24,256]{3,2,1,0:T(8,128)(2,1)}), bf16[4,16,24,256]{3,2,1,0:T(8,128)(2,1)S(1)}, u32[]{:S(2)}, u32[]{:S(2)}) async-start(bf16[4,16,24,256]{3,2,1,0:T(8,128)(2,1)} %bitcast.28), calls=%async_computation.3 | async-start | bytes 1572864 | tf_op jit(solution)/shard_map/all_to_all | solution.py:71
  266.5 40.6 %reduce-scatter.5.cloned.1.call-start = ((), (), s32[]{:S(2)}) async-start(), calls=%async_computation.7 | async-start | bytes 655360 | tf_op jit(solution)/shard_map/reduce_scatter | solution.py:66
  288.4 17.7 %all-to-all-start.3 = ((bf16[4,16,24,256]{3,2,1,0:T(8,128)(2,1)}), bf16[4,16,24,256]{3,2,1,0:T(8,128)(2,1)S(1)}, u32[]{:S(2)}, u32[]{:S(2)}) async-start(bf16[4,16,24,256]{3,2,1,0:T(8,128)(2,1)} %copy.52), calls=%async_computation.4 | async-start | bytes 1572864 | tf_op jit(solution)/shard_map/all_to_all | solution.py:76
Sparse Core Ops, SparseCore 0:
  183.0 20.9 reduce-scatter.2
  282.9 20.9 reduce-scatter.4
where the time goes:
time: 316 us; the launch traced here: 315 us
  matrix products  121 us (38%)
  local copies, waits for them, and re-layouts  101 us (32%)
  blocking collectives  29.4 us (9%)
  waiting for transfers between devices  27.5 us (9%)
  starting transfers between devices  15.3 us (5%)
  between operations  13.9 us (4%)
  other arithmetic  7.21 us (2%)
    squeeze x1, local copies, waits for them, and re-layouts, device_step(): cache[layer_idx]  97 us
    dot_general x2, matrix products, local_attention(): jnp.einsum('bht,btc->bhc', probs, cache_l[:, :, :LATENT], preferred_eleme...  51.2 us
    dot_general x2, matrix products, local_attention(): jnp.einsum('bhc,btc->bht', queries, cache_l, preferred_element_type=jnp.f...  50.6 us
    all_gather x2, blocking collectives, device_step(): gathered = lax.all_gather(ffn_in, 'dp', axis=0, tiled=True)  29.4 us
    all_to_all x2, waiting for transfers between devices, device_step(): returned = lax.all_to_all(expert_out, 'dp', 0, 0, tiled=True)  27.4 us
    all_to_all x2, starting transfers between devices, device_step(): recv_buf = lax.all_to_all(send_buf, 'dp', 0, 0, tiled=True)  8.1 us
    all_to_all x2, starting transfers between devices, device_step(): returned = lax.all_to_all(expert_out, 'dp', 0, 0, tiled=True)  7.17 us
  transfers between devices with their start and end apart: 6, of which 2 were waited for; matrix products, arithmetic and copies ran while one was open for 5% of the time, Pallas kernels for 0%

commit v1 on v0

--- a/solution.py
+++ b/solution.py
@@ -1,37 +1,233 @@
+import functools
 import jax
 import jax.numpy as jnp
 from jax import lax
+from jax.experimental import pallas as pl
+from jax.experimental.pallas import tpu as pltpu
 from jax.sharding import PartitionSpec as P
 
 NORM_EPS = 1e-6
 ATT_SCALE = 1.0 / (192.0 ** 0.5)
 LATENT = 512
+CHUNK = 128
+F32 = jnp.float32
+BF16 = jnp.bfloat16
 
 
 def rms_norm(values):
-    vals32 = values.astype(jnp.float32)
+    vals32 = values.astype(F32)
     return vals32 * lax.rsqrt(jnp.mean(vals32 * vals32, axis=-1, keepdims=True) + NORM_EPS)
+
+
+def bucket_order(lengths):
+    count = lengths.shape[0]
+    chunks = (lengths + (CHUNK - 1)) // CHUNK
+    ids = jnp.arange(count, dtype=jnp.int32)
+    ahead = (chunks[None, :] > chunks[:, None]) | ((chunks[None, :] == chunks[:, None]) & (ids[None, :] < ids[:, None]))
+    place = jnp.sum(ahead.astype(jnp.int32), axis=1)
+    hit = place[None, :] == ids[:, None]
+    order = jnp.sum(jnp.where(hit, ids[None, :], 0), axis=1)
+    sorted_len = jnp.sum(jnp.where(hit, lengths[None, :], 0), axis=1)
+    return place, order, sorted_len
+
+
+def attn_kernel(layer, slots, order_ref, slen_ref, place_ref, x_ref, cache_ref, wq_hbm, wo_hbm,
+                x_out, g_out, wq, wo, buf, qbd, obuf, pbuf, sem, wsem):
+    toks, d_model = x_ref.shape
+    kv_dim, seq_len = cache_ref.shape[2], cache_ref.shape[3]
+    rope = kv_dim - LATENT
+    groups = toks // 8
+    max_n = seq_len // CHUNK
+
+    def group_n(g):
+        return lax.div(slen_ref[g * 8] + (CHUNK - 1), CHUNK)
+
+    def start_group(g):
+        slot = lax.rem(g, slots)
+        n = group_n(g)
+        for nn in range(1, max_n + 1):
+            @pl.when(n == nn)
+            def _():
+                for i in range(8):
+                    b = order_ref[g * 8 + i]
+                    half, j = i // 4, i % 4
+                    cols = pl.ds(0, nn * CHUNK)
+                    pltpu.make_async_copy(
+                        cache_ref.at[layer, b, pl.ds(0, LATENT), cols],
+                        buf.at[slot, half, pl.ds(j * LATENT, LATENT), cols], sem.at[slot]).start()
+                    pltpu.make_async_copy(
+                        cache_ref.at[layer, b, pl.ds(LATENT, rope), cols],
+                        buf.at[slot, half, pl.ds(4 * LATENT + j * rope, rope), cols], sem.at[slot]).start()
+
+    wq_copy = pltpu.make_async_copy(wq_hbm.at[layer], wq, wsem.at[0])
+    wo_copy = pltpu.make_async_copy(wo_hbm.at[layer], wo, wsem.at[1])
+    wq_copy.start()
+    for g in range(slots):
+        start_group(g)
+    wo_copy.start()
+
+    rows = 2 * toks
+    row_id = lax.broadcasted_iota(jnp.int32, (rows, toks), 0)
+    place = place_ref[...]
+    base = lax.shift_right_logical(place, 2) * 8 + lax.rem(place, 4)
+    pick0 = (row_id == base).astype(BF16)
+    pick1 = (row_id == base + 4).astype(BF16)
+    h = rms_norm(x_ref[...]).astype(BF16)
+    wq_copy.wait()
+    q = jnp.dot(h, wq[...], preferred_element_type=F32).astype(BF16)
+    qrows = (jnp.dot(pick0, q[:, :kv_dim], preferred_element_type=F32)
+             + jnp.dot(pick1, q[:, kv_dim:], preferred_element_type=F32))
+    sub = lax.rem(lax.broadcasted_iota(jnp.int32, (rows, 1), 0), 4)
+    for j in range(4):
+        qbd[:, j * LATENT:(j + 1) * LATENT] = jnp.where(sub == j, qrows[:, :LATENT], 0.0).astype(BF16)
+    tail = qrows[:, LATENT:]
+    tail2 = jnp.concatenate([tail, tail], axis=1)
+    lane = lax.broadcasted_iota(jnp.int32, (rows, 2 * rope), 1)
+    for jj in range(2):
+        keep = sub == (2 * jj + (lane >= rope).astype(jnp.int32))
+        qbd[:, 4 * LATENT + jj * 2 * rope:4 * LATENT + (jj + 1) * 2 * rope] = jnp.where(keep, tail2, 0.0).astype(BF16)
+
+    row16 = lax.broadcasted_iota(jnp.int32, (16, CHUNK), 0)
+    sub16 = lax.rem(row16, 4)
+    lane16 = lax.broadcasted_iota(jnp.int32, (16, CHUNK), 1)
+    half16 = (row16 >= 8).astype(jnp.int32)
+    seq16 = half16 * 4 + sub16
+
+    def scores(g, nn):
+        slot = lax.rem(g, slots)
+        lhs = qbd[pl.ds(pl.multiple_of(g * 16, 16), 16), :]
+        lens = jnp.zeros((16, CHUNK), jnp.int32)
+        for i in range(8):
+            lens = jnp.where(seq16 == i, slen_ref[g * 8 + i], lens)
+        out = []
+        for k in range(nn):
+            cols = pl.ds(k * CHUNK, CHUNK)
+            rhs = jnp.concatenate([buf[slot, 0, :, cols], buf[slot, 1, :, cols]], axis=1)
+            raw = jnp.dot(lhs, rhs, preferred_element_type=F32)
+            s = jnp.concatenate([raw[0:8, :CHUNK], raw[8:16, CHUNK:]], axis=0) * ATT_SCALE
+            out.append(jnp.where(lane16 + k * CHUNK < lens, s, -jnp.inf))
+        return out
+
+    def softmax(s):
+        m = s[0]
+        for t in s[1:]:
+            m = jnp.maximum(m, t)
+        m = jnp.max(m, axis=1, keepdims=True)
+        e = [jnp.exp(t - m) for t in s]
+        tot = e[0]
+        for t in e[1:]:
+            tot = tot + t
+        inv = 1.0 / jnp.sum(tot, axis=1, keepdims=True)
+        return [(t * inv) for t in e]
+
+    def values(g, p):
+        slot = lax.rem(g, slots)
+        lhs, rhs = [], []
+        for k, t in enumerate(p):
+            cols = pl.ds(k * CHUNK, CHUNK)
+            for j in range(4):
+                for half in range(2):
+                    keep = (sub16 == j) & (half16 == half)
+                    lhs.append(jnp.where(keep, t, 0.0).astype(BF16))
+                    rhs.append(buf[slot, half, pl.ds(j * LATENT, LATENT), cols])
+        o = lax.dot_general(jnp.concatenate(lhs, axis=1), jnp.concatenate(rhs, axis=1),
+                            (((1,), (1,)), ((), ())), preferred_element_type=F32)
+        obuf[pl.ds(pl.multiple_of(g * 16, 16), 16), :] = o.astype(BF16)
+
+    def wait_group(g, nn):
+        slot = lax.rem(g, slots)
+        view = buf.at[slot, :, :, pl.ds(0, nn * CHUNK)]
+        pltpu.make_async_copy(view, view, sem.at[slot]).wait()
+
+    def stage_scores(g, nn):
+        p = softmax(scores(g, nn))
+        for k, t in enumerate(p):
+            pbuf[lax.rem(g, 2), k] = t
+
+    def stage_values(g, nn):
+        values(g, [pbuf[lax.rem(g, 2), k] for k in range(nn)])
+
+    def each_n(n, fn):
+        for nn in range(1, max_n + 1):
+            pl.when(n == nn)(functools.partial(fn, nn))
+
+    def first(nn):
+        wait_group(0, nn)
+        stage_scores(0, nn)
+    each_n(group_n(0), first)
+
+    def body(g, _):
+        n_prev = group_n(g - 1)
+        n_cur = group_n(g)
+
+        @pl.when(n_prev == n_cur)
+        def _():
+            def both(nn):
+                wait_group(g, nn)
+                p_prev = [pbuf[lax.rem(g - 1, 2), k] for k in range(nn)]
+                s = scores(g, nn)
+                values(g - 1, p_prev)
+                for k, t in enumerate(softmax(s)):
+                    pbuf[lax.rem(g, 2), k] = t
+            each_n(n_cur, both)
+
+        @pl.when(n_prev != n_cur)
+        def _():
+            each_n(n_prev, functools.partial(stage_values, g - 1))
+            def only(nn):
+                wait_group(g, nn)
+                stage_scores(g, nn)
+            each_n(n_cur, only)
+
+        @pl.when(g - 1 + slots < groups)
+        def _():
+            start_group(g - 1 + slots)
+        return 0
+
+    lax.fori_loop(1, groups, body, 0)
+    each_n(group_n(groups - 1), functools.partial(stage_values, groups - 1))
+
+    wo_copy.wait()
+    picked = obuf[...]
+    total = x_ref[...].astype(F32)
+    for head, pick in enumerate((pick0, pick1)):
+        o = lax.dot_general(pick, picked, (((0,), (0,)), ((), ())), preferred_element_type=F32).astype(BF16)
+        total = total + jnp.dot(o, wo[head * LATENT:(head + 1) * LATENT, :], preferred_element_type=F32)
+    x_new = total.astype(BF16)
+    x_out[...] = x_new
+    g_out[...] = rms_norm(x_new).astype(BF16)
+
+
+def attention(layer, place, order, sorted_len, x, cache_t, w_q, w_o, slots=8):
+    toks, d_model = x.shape
+    kv_dim, seq_len = cache_t.shape[2], cache_t.shape[3]
+    any_spec = pl.BlockSpec(memory_space=pl.ANY)
+    smem = pl.BlockSpec(memory_space=pltpu.SMEM)
+    vmem = pl.BlockSpec(memory_space=pltpu.VMEM)
+    return pl.pallas_call(
+        functools.partial(attn_kernel, layer, slots),
+        out_shape=(jax.ShapeDtypeStruct((toks, d_model), BF16), jax.ShapeDtypeStruct((toks, d_model), BF16)),
+        in_specs=[smem, smem, vmem, vmem, any_spec, any_spec, any_spec],
+        out_specs=(vmem, vmem),
+        scratch_shapes=[
+            pltpu.VMEM(w_q.shape[1:], BF16),
+            pltpu.VMEM(w_o.shape[1:], BF16),
+            pltpu.VMEM((slots, 2, 4 * kv_dim, seq_len), BF16),
+            pltpu.VMEM((2 * toks, 4 * kv_dim), BF16),
+            pltpu.VMEM((2 * toks, LATENT), BF16),
+            pltpu.VMEM((2, seq_len // CHUNK, 16, CHUNK), F32),
+            pltpu.SemaphoreType.DMA((slots,)),
+            pltpu.SemaphoreType.DMA((2,)),
+        ],
+        compiler_params=pltpu.CompilerParams(vmem_limit_bytes=48 * 1024 * 1024),
+        name="latent_attention",
+    )(order, sorted_len, place.reshape(1, toks), x, cache_t, w_q, w_o)
 
 
 def gated_hidden(tok_in, w_up, w_gate):
     gate_in = jnp.dot(tok_in, w_gate, preferred_element_type=jnp.float32)
     up_in = jnp.dot(tok_in, w_up, preferred_element_type=jnp.float32)
     return (jax.nn.silu(gate_in) * up_in).astype(jnp.bfloat16)
-
-
-def local_attention(resid, lengths, cache_l, w_q_l, w_o_l):
-    tok_count = resid.shape[0]
-    seq_len, kv_dim = cache_l.shape[1], cache_l.shape[2]
-    num_heads = w_q_l.shape[1] // kv_dim
-    normed = rms_norm(resid).astype(jnp.bfloat16)
-    queries = jnp.dot(normed, w_q_l, preferred_element_type=jnp.float32).astype(jnp.bfloat16)
-    queries = queries.reshape(tok_count, num_heads, kv_dim)
-    scores = jnp.einsum('bhc,btc->bht', queries, cache_l, preferred_element_type=jnp.float32) * ATT_SCALE
-    valid = jnp.arange(seq_len)[None, None, :] < lengths[:, None, None]
-    probs = jax.nn.softmax(jnp.where(valid, scores, -jnp.inf), axis=-1).astype(jnp.bfloat16)
-    attn = jnp.einsum('bht,btc->bhc', probs, cache_l[:, :, :LATENT], preferred_element_type=jnp.float32)
-    attn = attn.astype(jnp.bfloat16).reshape(tok_count, num_heads * LATENT)
-    return (resid.astype(jnp.float32) + jnp.dot(attn, w_o_l, preferred_element_type=jnp.float32)).astype(jnp.bfloat16)
 
 
 def route_select(ids_l, slot_l, experts, capacity):
@@ -57,9 +253,10 @@
         top_k = expert_ids.shape[2]
         capacity = max(1, (2 * batch_dev * top_k) // experts)
         resid = x
+        place, order, sorted_len = bucket_order(lengths)
+        cache_t = jnp.swapaxes(cache, 2, 3)
         for layer_idx in range(cache.shape[0]):
-            resid = local_attention(resid, lengths, cache[layer_idx], w_q[layer_idx], w_o[layer_idx])
-            ffn_in = rms_norm(resid).astype(jnp.bfloat16)
+            resid, ffn_in = attention(layer_idx, place, order, sorted_len, resid, cache_t, w_q, w_o)
             gathered = lax.all_gather(ffn_in, 'dp', axis=0, tiled=True)
             shared_h = gated_hidden(gathered, w1_sh[layer_idx], w3_sh[layer_idx])
             shared_part = jnp.dot(shared_h, w2_sh[layer_idx], preferred_element_type=jnp.float32)

time: 316 us -> 170 us (0.54)
  matrix products: 121 us -> 18.3 us
  local copies, waits for them, and re-layouts: 101 us -> 6.95 us
  Pallas kernels: 0 us -> 52.9 us
    dot_general x8 -> x0, matrix products: 104 us -> none  [the longest x2 51.2 us: local_attention(): jnp.einsum('bht,btc->bhc', probs, cache_l[:, :, :LATENT], preferred_eleme...]
    squeeze x1 -> x0, local copies, waits for them, and re-layouts: 97 us -> none  [device_step(): cache[layer_idx]]
    pallas_call x0 -> x2, Pallas kernels: none -> 52.9 us  [attention(): pl.pallas_call(functools.partial(attn_kernel, layer, slots), out_shape=(j...]
    unnamed x26 -> x22, local copies, waits for them, and re-layouts: 0.14 us -> 4.26 us
  transfers between devices with their start and end apart: 6 -> 6, of which waited for: 2 -> 2; matrix products, arithmetic and copies ran while one was open for 5% -> 11% of each run, Pallas kernels for 0% -> 0%
where the time goes in v1:
time: 170 us; the launch traced here: 169 us
  Pallas kernels  52.9 us (31%)
  blocking collectives  29.4 us (17%)
  waiting for transfers between devices  27.7 us (16%)
  matrix products  18.3 us (11%)
  starting transfers between devices  14.7 us (9%)
  between operations  13.7 us (8%)
  local copies, waits for them, and re-layouts  6.95 us (4%)
  other arithmetic  5.52 us (3%)
    pallas_call x2, Pallas kernels, attention(): pl.pallas_call(functools.partial(attn_kernel, layer, slots), out_shape=(j...  52.9 us
    all_gather x2, blocking collectives, device_step(): gathered = lax.all_gather(ffn_in, 'dp', axis=0, tiled=True)  29.4 us
    all_to_all x2, waiting for transfers between devices, device_step(): returned = lax.all_to_all(expert_out, 'dp', 0, 0, tiled=True)  27.6 us
    all_to_all x2, starting transfers between devices, device_step(): recv_buf = lax.all_to_all(send_buf, 'dp', 0, 0, tiled=True)  7.7 us
    all_to_all x2, starting transfers between devices, device_step(): returned = lax.all_to_all(expert_out, 'dp', 0, 0, tiled=True)  6.99 us
    dot_general x2, matrix products, device_step(): jnp.einsum('nscf,nfd->sncd', hidden, w2_exp[layer_idx], preferred_element...  5.52 us
    unnamed x22, local copies, waits for them, and re-layouts  4.26 us
    dot_general x2, matrix products, device_step(): jnp.einsum('sncd,ndf->nscf', recv_buf, w3_exp[layer_idx], preferred_eleme...  3.95 us
  transfers between devices with their start and end apart: 6, of which 2 were waited for; matrix products, arithmetic and copies ran while one was open for 11% of the time, Pallas kernels for 0%

profile of v1, /device:TPU:0, one launch (start us, length us, event | category | flops | bytes accessed | tf_op | source)
XLA Modules:
  0.0 169.1 jit_solution(637204222320984104)
XLA Ops:
  7.4 0.8 select_reduce_fusion
  8.1 0.8 fusion.97
  9.0 0.7 fusion.4
  9.7 1.3 copy-done
  10.9 1.2 copy-done.2
  12.2 0.8 copy-done.4
  13.0 26.4 %latent_attention.2 = (bf16[128,256]{1,0:T(8,128)(2,1)S(1)}, bf16[128,256]{1,0:T(8,128)(2,1)S(1)}) custom-call(s32[128]{0:T(128)S(1)} %get-tuple-element.14.order_ref, s32[128]{0:T(128)S(1)} %get-tuple-element.13.slen_ref, s32[1,128]{1,0:T(1,128)S(1)} %bitcast.102, bf16[128,256]{1,0:T(8,128)(2,1)S(1)} %copy-done.4, ...), custom_call_target="tpu_custom_call" | custom-call | tf_op jit(solution)/shard_map/latent_attention/pallas_call | solution.py:207
  39.5 1.3 convolution_convert_fusion.1
  40.7 4.2 %all-to-all-start = ((bf16[4,16,24,256]{3,2,1,0:T(8,128)(2,1)}), bf16[4,16,24,256]{3,2,1,0:T(8,128)(2,1)S(1)}, u32[]{:S(2)}, u32[]{:S(2)}) async-start(bf16[4,16,24,256]{3,2,1,0:T(8,128)(2,1)} %bitcast.4), calls=%async_computation | async-start | bytes 1572864 | tf_op jit(solution)/shard_map/all_to_all | solution.py:268
  45.0 14.8 %all_gather.6 = bf16[512,256]{1,0:T(8,128)(2,1)S(1)} all-gather(bf16[128,256]{1,0:T(8,128)(2,1)S(1)} %get-tuple-element.10), channel_id=1, replica_groups=mesh['replica'=2,'dp'=4] {'dp'}, dimensions={0}, use_global_device_ids=true | all-gather | bytes 327680 | tf_op jit(solution)/shard_map/all_gather | solution.py:260
  60.0 1.3 fusion.43
  61.3 2.0 %fusion.16 = f32[16,4,24,176]{3,2,1,0:T(8,128)S(1)} fusion(bf16[2,16,256,176]{2,3,1,0:T(8,128)(2,1)} %param.23, bf16[4,16,24,256]{3,2,1,0:T(8,128)(2,1)S(1)} %all-to-all-done), kind=kOutput, calls=%fused_computation.22 | convolution fusion | flops 138412032 | bytes 3309568 | tf_op jit(solution)/shard_map/sncd,ndf->nscf/dot_general | solution.py:269
  63.3 2.8 %fusion.35 = bf16[4,16,24,256]{3,2,0,1:T(8,128)(2,1)S(1)} fusion(bf16[2,16,176,256]{3,2,1,0:T(8,128)(2,1)} %param.24, f32[16,4,24,176]{3,2,1,0:T(8,128)S(1)} %fusion.16, bf16[2,16,256,176]{2,3,1,0:T(8,128)(2,1)} %param.22, bf16[4,16,24,256]{3,2,1,0:T(8,128)(2,1)S(1)} %all-to-all-done), kind=kOutput, calls=%fused_computation.35 | convolution fusion | flops 278839296 | bytes 5537792 | tf_op jit(solution)/shard_map/nscf,nfd->sncd/dot_general | solution.py:272
  66.1 0.9 copy.44
  67.0 3.5 %all-to-all-start.1 = ((bf16[4,16,24,256]{3,2,1,0:T(8,128)(2,1)}), bf16[4,16,24,256]{3,2,1,0:T(8,128)(2,1)S(1)}, u32[]{:S(2)}, u32[]{:S(2)}) async-start(bf16[4,16,24,256]{3,2,1,0:T(8,128)(2,1)} %copy.44), calls=%async_computation.1 | async-start | bytes 1572864 | tf_op jit(solution)/shard_map/all_to_all | solution.py:273
  70.6 0.7 fusion.5
  71.3 13.4 %all-to-all-done.1 = bf16[4,16,24,256]{3,2,1,0:T(8,128)(2,1)S(1)} async-done(((bf16[4,16,24,256]{3,2,1,0:T(8,128)(2,1)}), bf16[4,16,24,256]{3,2,1,0:T(8,128)(2,1)S(1)}, u32[]{:S(2)}, u32[]{:S(2)}) %all-to-all-start.1) | async-done | bytes 786464 | tf_op jit(solution)/shard_map/all_to_all | solution.py:273
  84.7 0.9 copy-done.5
  85.6 2.3 %fusion.39 = f32[128,256]{1,0:T(8,128)S(1)} fusion(bf16[1536,256,1]{1,0,2:T(8,128)(2,1)} %bitcast.104, s32[128,6]{0,1:T(8,128)S(1)} %fusion.89, f32[128,6]{0,1:T(8,128)S(1)} %bitcast.106), kind=kOutput, calls=%fused_computation.37 | convolution fusion | flops 605519872 | bytes 923648 | tf_op jit(solution)/shard_map/cls,se->cle/dot_general | solution.py:275
  87.9 0.9 add_convert_fusion.1.x_ref
  88.8 26.5 %latent_attention.3 = (bf16[128,256]{1,0:T(8,128)(2,1)S(1)}, bf16[128,256]{1,0:T(8,128)(2,1)S(1)}) custom-call(s32[128]{0:T(128)S(1)} %get-tuple-element.14.order_ref, s32[128]{0:T(128)S(1)} %get-tuple-element.13.slen_ref, s32[1,128]{1,0:T(1,128)S(1)} %bitcast.103, bf16[128,256]{1,0:T(8,128)(2,1)S(1)} %add_convert_fusion.1.x_ref, ...), custom_call_target="tpu_custom_call" | custom-call | tf_op jit(solution)/shard_map/latent_attention/pallas_call | solution.py:207
  115.3 1.3 convolution_convert_fusion
  116.6 3.5 %all-to-all-start.2 = ((bf16[4,16,24,256]{3,2,1,0:T(8,128)(2,1)}), bf16[4,16,24,256]{3,2,1,0:T(8,128)(2,1)S(1)}, u32[]{:S(2)}, u32[]{:S(2)}) async-start(bf16[4,16,24,256]{3,2,1,0:T(8,128)(2,1)} %bitcast.22), calls=%async_computation.3 | async-start | bytes 1572864 | tf_op jit(solution)/shard_map/all_to_all | solution.py:268
  120.1 14.7 %all_gather.7 = bf16[512,256]{1,0:T(8,128)(2,1)S(1)} all-gather(bf16[128,256]{1,0:T(8,128)(2,1)S(1)} %get-tuple-element.12), channel_id=1, replica_groups=mesh['replica'=2,'dp'=4] {'dp'}, dimensions={0}, use_global_device_ids=true | all-gather | bytes 327680 | tf_op jit(solution)/shard_map/all_gather | solution.py:260
  135.0 1.3 fusion.42
  136.4 2.0 %fusion.11 = f32[16,4,24,176]{3,2,1,0:T(8,128)S(1)} fusion(bf16[2,16,256,176]{2,3,1,0:T(8,128)(2,1)} %param.23, bf16[4,16,24,256]{3,2,1,0:T(8,128)(2,1)S(1)} %all-to-all-done.2), kind=kOutput, calls=%fused_computation.17 | convolution fusion | flops 138412032 | bytes 3309568 | tf_op jit(solution)/shard_map/sncd,ndf->nscf/dot_general | solution.py:269
  138.4 2.8 %fusion.32 = bf16[4,16,24,256]{3,2,0,1:T(8,128)(2,1)S(1)} fusion(bf16[2,16,176,256]{3,2,1,0:T(8,128)(2,1)} %param.24, f32[16,4,24,176]{3,2,1,0:T(8,128)S(1)} %fusion.11, bf16[2,16,256,176]{2,3,1,0:T(8,128)(2,1)} %param.22, bf16[4,16,24,256]{3,2,1,0:T(8,128)(2,1)S(1)} %all-to-all-done.2), kind=kOutput, calls=%fused_computation.34 | convolution fusion | flops 278839296 | bytes 5537792 | tf_op jit(solution)/shard_map/nscf,nfd->sncd/dot_general | solution.py:272
  141.1 0.9 copy.50
  142.1 3.5 %all-to-all-start.3 = ((bf16[4,16,24,256]{3,2,1,0:T(8,128)(2,1)}), bf16[4,16,24,256]{3,2,1,0:T(8,128)(2,1)S(1)}, u32[]{:S(2)}, u32[]{:S(2)}) async-start(bf16[4,16,24,256]{3,2,1,0:T(8,128)(2,1)} %copy.50), calls=%async_computation.4 | async-start | bytes 1572864 | tf_op jit(solution)/shard_map/all_to_all | solution.py:273
  145.6 14.2 %all-to-all-done.3 = bf16[4,16,24,256]{3,2,1,0:T(8,128)(2,1)S(1)} async-done(((bf16[4,16,24,256]{3,2,1,0:T(8,128)(2,1)}), bf16[4,16,24,256]{3,2,1,0:T(8,128)(2,1)S(1)}, u32[]{:S(2)}, u32[]{:S(2)}) %all-to-all-start.3) | async-done | bytes 786464 | tf_op jit(solution)/shard_map/all_to_all | solution.py:273
  159.8 1.0 fusion.38
  160.7 1.6 add_convert_fusion
  (33 shorter events, 1.4 us)
Async XLA Ops:
  9.7 1.3 copy-start
  10.9 1.2 copy-start.2
  12.2 0.8 copy-start.4
  39.4 20.3 %copy-start.6 = (bf16[2,256,88]{1,2,0:T(8,128)(2,1)S(1)}, bf16[2,256,88]{1,2,0:T(8,128)(2,1)}, u32[]{:S(2)}) copy-start(bf16[2,256,88]{1,2,0:T(8,128)(2,1)} %param.26) | copy-start | bytes 270340
  39.4 20.5 %copy-start.8 = (bf16[2,88,256]{2,1,0:T(8,128)(2,1)S(1)}, bf16[2,88,256]{2,1,0:T(8,128)(2,1)}, u32[]{:S(2)}) copy-start(bf16[2,88,256]{2,1,0:T(8,128)(2,1)} %param.27) | copy-start | bytes 270340
  39.5 20.5 %copy-start.9 = (bf16[2,256,88]{1,2,0:T(8,128)(2,1)S(1)}, bf16[2,256,88]{1,2,0:T(8,128)(2,1)}, u32[]{:S(2)}) copy-start(bf16[2,256,88]{1,2,0:T(8,128)(2,1)} %param.25) | copy-start | bytes 270340
  40.7 20.5 %all-to-all-start = ((bf16[4,16,24,256]{3,2,1,0:T(8,128)(2,1)}), bf16[4,16,24,256]{3,2,1,0:T(8,128)(2,1)S(1)}, u32[]{:S(2)}, u32[]{:S(2)}) async-start(bf16[4,16,24,256]{3,2,1,0:T(8,128)(2,1)} %bitcast.4), calls=%async_computation | async-start | bytes 1572864 | tf_op jit(solution)/shard_map/all_to_all | solution.py:268
  45.0 42.9 %reduce-scatter.3.cloned.1.call-start = ((), (), s32[]{:S(2)}) async-start(), calls=%async_computation.6 | async-start | bytes 655360 | tf_op jit(solution)/shard_map/reduce_scatter | solution.py:263
  66.0 4.5 %copy-start.7 = (f32[2,128,6]{1,0,2:T(2,128)S(1)}, f32[2,128,6]{1,0,2:T(2,128)}, u32[]{:S(2)}) copy-start(f32[2,128,6]{1,0,2:T(2,128)} %param.21) | copy-start | bytes 18436
  67.0 17.7 %all-to-all-start.1 = ((bf16[4,16,24,256]{3,2,1,0:T(8,128)(2,1)}), bf16[4,16,24,256]{3,2,1,0:T(8,128)(2,1)S(1)}, u32[]{:S(2)}, u32[]{:S(2)}) async-start(bf16[4,16,24,256]{3,2,1,0:T(8,128)(2,1)} %copy.44), calls=%async_computation.1 | async-start | bytes 1572864 | tf_op jit(solution)/shard_map/all_to_all | solution.py:273
  84.7 0.9 copy-start.5
  85.6 3.2 %copy-start.1 = (bf16[2,256,1152]{2,1,0:T(8,128)(2,1)S(1)}, bf16[2,256,1152]{2,1,0:T(8,128)(2,1)}, u32[]{:S(2)}) copy-start(bf16[2,256,1152]{2,1,0:T(8,128)(2,1)} %wq_hbm.3) | copy-start | bytes 3538948
  85.6 3.2 %copy-start.3 = (bf16[2,1024,256]{2,1,0:T(8,128)(2,1)S(1)}, bf16[2,1024,256]{2,1,0:T(8,128)(2,1)}, u32[]{:S(2)}) copy-start(bf16[2,1024,256]{2,1,0:T(8,128)(2,1)} %wo_hbm.3) | copy-start | bytes 3145732
  116.6 19.8 %all-to-all-start.2 = ((bf16[4,16,24,256]{3,2,1,0:T(8,128)(2,1)}), bf16[4,16,24,256]{3,2,1,0:T(8,128)(2,1)S(1)}, u32[]{:S(2)}, u32[]{:S(2)}) async-start(bf16[4,16,24,256]{3,2,1,0:T(8,128)(2,1)} %bitcast.22), calls=%async_computation.3 | async-start | bytes 1572864 | tf_op jit(solution)/shard_map/all_to_all | solution.py:268
  120.1 40.6 %reduce-scatter.5.cloned.1.call-start = ((), (), s32[]{:S(2)}) async-start(), calls=%async_computation.7 | async-start | bytes 655360 | tf_op jit(solution)/shard_map/reduce_scatter | solution.py:263
  142.1 17.7 %all-to-all-start.3 = ((bf16[4,16,24,256]{3,2,1,0:T(8,128)(2,1)}), bf16[4,16,24,256]{3,2,1,0:T(8,128)(2,1)S(1)}, u32[]{:S(2)}, u32[]{:S(2)}) async-start(bf16[4,16,24,256]{3,2,1,0:T(8,128)(2,1)} %copy.50), calls=%async_computation.4 | async-start | bytes 1572864 | tf_op jit(solution)/shard_map/all_to_all | solution.py:273
Sparse Core Ops, SparseCore 0:
  61.4 20.7 reduce-scatter.2
  136.5 19.9 reduce-scatter.4

commit v2 on v1

--- a/solution.py
+++ b/solution.py
@@ -32,7 +32,7 @@
 
 
 def attn_kernel(layer, slots, order_ref, slen_ref, place_ref, x_ref, cache_ref, wq_hbm, wo_hbm,
-                x_out, g_out, wq, wo, buf, qbd, obuf, pbuf, sem, wsem):
+                ids_ref, slot_ref, route_ref, x_out, g_out, wt_out, wq, wo, buf, qbd, obuf, pbuf, sem, wsem):
     toks, d_model = x_ref.shape
     kv_dim, seq_len = cache_ref.shape[2], cache_ref.shape[3]
     rope = kv_dim - LATENT
@@ -65,6 +65,15 @@
     for g in range(slots):
         start_group(g)
     wo_copy.start()
+
+    experts = wt_out.shape[0]
+    expert_id = lax.broadcasted_iota(jnp.int32, (experts, toks), 0)
+    wt = jnp.zeros((experts, toks), F32)
+    for j in range(ids_ref.shape[0]):
+        at = pl.ds(layer, 1)
+        hit = (ids_ref[j, at, :] == expert_id) & (slot_ref[j, at, :] >= 0)
+        wt = wt + jnp.where(hit, route_ref[j, at, :], 0.0)
+    wt_out[...] = wt
 
     rows = 2 * toks
     row_id = lax.broadcasted_iota(jnp.int32, (rows, toks), 0)
@@ -198,7 +207,7 @@
     g_out[...] = rms_norm(x_new).astype(BF16)
 
 
-def attention(layer, place, order, sorted_len, x, cache_t, w_q, w_o, slots=8):
+def attention(layer, place, order, sorted_len, x, cache_t, w_q, w_o, ids, slot, route_w, experts, slots=8):
     toks, d_model = x.shape
     kv_dim, seq_len = cache_t.shape[2], cache_t.shape[3]
     any_spec = pl.BlockSpec(memory_space=pl.ANY)
@@ -206,9 +215,10 @@
     vmem = pl.BlockSpec(memory_space=pltpu.VMEM)
     return pl.pallas_call(
         functools.partial(attn_kernel, layer, slots),
-        out_shape=(jax.ShapeDtypeStruct((toks, d_model), BF16), jax.ShapeDtypeStruct((toks, d_model), BF16)),
-        in_specs=[smem, smem, vmem, vmem, any_spec, any_spec, any_spec],
-        out_specs=(vmem, vmem),
+        out_shape=(jax.ShapeDtypeStruct((toks, d_model), BF16), jax.ShapeDtypeStruct((toks, d_model), BF16),
+                   jax.ShapeDtypeStruct((experts, toks), F32)),
+        in_specs=[smem, smem, vmem, vmem, any_spec, any_spec, any_spec, vmem, vmem, vmem],
+        out_specs=(vmem, vmem, vmem),
         scratch_shapes=[
             pltpu.VMEM(w_q.shape[1:], BF16),
             pltpu.VMEM(w_o.shape[1:], BF16),
@@ -221,22 +231,144 @@
         ],
         compiler_params=pltpu.CompilerParams(vmem_limit_bytes=48 * 1024 * 1024),
         name="latent_attention",
-    )(order, sorted_len, place.reshape(1, toks), x, cache_t, w_q, w_o)
-
-
-def gated_hidden(tok_in, w_up, w_gate):
-    gate_in = jnp.dot(tok_in, w_gate, preferred_element_type=jnp.float32)
-    up_in = jnp.dot(tok_in, w_up, preferred_element_type=jnp.float32)
-    return (jax.nn.silu(gate_in) * up_in).astype(jnp.bfloat16)
-
-
-def route_select(ids_l, slot_l, experts, capacity):
-    buf_rows = jnp.where(slot_l >= 0, ids_l * capacity + slot_l, -1)
-    return (buf_rows[:, :, None] == jnp.arange(experts * capacity)).astype(jnp.bfloat16)
+    )(order, sorted_len, place.reshape(1, toks), x, cache_t, w_q, w_o, ids, slot, route_w)
+
+
+MESH_ID = pl.DeviceIdType.MESH
+EXP_STEP = 4
+
+
+def moe_kernel(layer, x_ref, g_ref, route_ref, w1_hbm, w3_hbm, w2_hbm, w1s_hbm, w3s_hbm, w2s_hbm, out_ref,
+               gall, wall, w1, w3, w2, w2t, w1s, w3s, w2s, acc, part, wsem, gsend, grecv, rsend, rrecv, psend, precv):
+    me = lax.axis_index('dp')
+    core = lax.rem(me, 2)
+    chip = lax.div(me, 2)
+    partner = chip * 2 + (1 - core)
+    cross = (1 - chip) * 2 + (1 - core)
+    same = (1 - chip) * 2 + core
+    peers = (partner, cross, same)
+    experts, ff, d_model = w2.shape
+    toks = x_ref.shape[0]
+
+    loads = [pltpu.make_async_copy(src.at[layer], dst, wsem.at[i]) for i, (src, dst) in enumerate(
+        ((w2_hbm, w2), (w1_hbm, w1), (w3_hbm, w3), (w1s_hbm, w1s), (w3s_hbm, w3s), (w2s_hbm, w2s)))]
+    for c in loads:
+        c.start()
+
+    barrier = pltpu.get_barrier_semaphore()
+    for p in peers:
+        pl.semaphore_signal(barrier, inc=1, device_id={'dp': p}, device_id_type=MESH_ID)
+    pl.semaphore_wait(barrier, 3)
+
+    gcopies, rcopies = [], []
+    for i, p in enumerate(peers):
+        rcopies.append(pltpu.make_async_remote_copy(
+            route_ref.at[pl.ds(p * experts, experts)], wall.at[i + 1], rsend.at[i], rrecv.at[i],
+            device_id={'dp': p}, device_id_type=MESH_ID))
+        gcopies.append(pltpu.make_async_remote_copy(
+            g_ref, gall.at[i + 1], gsend.at[i], grecv.at[i], device_id={'dp': p}, device_id_type=MESH_ID))
+    for i in range(3):
+        rcopies[i].start()
+        gcopies[i].start()
+
+    gall[0] = g_ref[...]
+    wall[0] = route_ref[pl.ds(pl.multiple_of(me * experts, experts), experts), :]
+    for c in loads:
+        c.wait()
+
+    def flip(e, carry):
+        w2t[e] = w2[e].T
+        return carry
+    lax.fori_loop(0, experts, flip, 0)
+    w2st = w2s[...].T
+
+    def gated(w3_rows, w1_rows, tok):
+        dims = (((1,), (1,)), ((), ()))
+        gate = lax.dot_general(w3_rows, tok, dims, preferred_element_type=F32)
+        up = lax.dot_general(w1_rows, tok, dims, preferred_element_type=F32)
+        return (gate * (1.0 / (1.0 + jnp.exp(-gate))) * up).astype(BF16)
+
+    def ffn(pair):
+        tok = jnp.concatenate([gall[2 * pair], gall[2 * pair + 1]], axis=0)
+        acc[pair] = jnp.dot(w2st, gated(w3s[...], w1s[...], tok), preferred_element_type=F32)
+
+        def step(s, carry):
+            rows = pl.ds(pl.multiple_of(s * (EXP_STEP * ff), 16), EXP_STEP * ff)
+            hid = gated(w3[rows, :], w1[rows, :], tok)
+            total = acc[pair]
+            for i in range(EXP_STEP):
+                e = s * EXP_STEP + i
+                u = jnp.dot(w2t[e], hid[i * ff:(i + 1) * ff], preferred_element_type=F32)
+                u = u.astype(BF16).astype(F32)
+                w = jnp.concatenate([wall[2 * pair, pl.ds(e, 1), :], wall[2 * pair + 1, pl.ds(e, 1), :]], axis=1)
+                total = total + jnp.where(w > 0.0, u * w, 0.0)
+            acc[pair] = total
+            return carry
+        lax.fori_loop(0, experts // EXP_STEP, step, 0)
+
+    def send_part(i, src, dst):
+        return pltpu.make_async_remote_copy(
+            src, part.at[i], psend.at[i], precv.at[i], device_id={'dp': dst}, device_id_type=MESH_ID)
+
+    rcopies[0].wait_recv()
+    gcopies[0].wait_recv()
+    ffn(0)
+    stage = acc.at[2, :, pl.ds(0, toks)]
+    home = send_part(0, acc.at[0, :, pl.ds(toks, toks)], partner)
+    home.start()
+
+    for i in (1, 2):
+        rcopies[i].wait_recv()
+        gcopies[i].wait_recv()
+    ffn(1)
+    relay = send_part(1, acc.at[1, :, pl.ds(0, toks)], partner)
+    relay.start()
+    relay.wait_recv()
+    acc[2, :, :toks] = acc[1, :, toks:] + part[1]
+    far = send_part(2, stage, same)
+    far.start()
+    home.wait_recv()
+    near = acc[0, :, :toks] + part[0]
+    far.wait_recv()
+    out_ref[...] = (x_ref[...].astype(F32) + (near + part[2]).T).astype(BF16)
+
+    for c in gcopies + rcopies + [home, relay, far]:
+        c.wait_send()
+
+
+def moe(layer, x, g, route, w1, w3, w2, w1s, w3s, w2s):
+    toks, d_model = x.shape
+    _, experts, ff, _ = w2.shape
+    shared = w2s.shape[1]
+    any_spec = pl.BlockSpec(memory_space=pl.ANY)
+    vmem = pl.BlockSpec(memory_space=pltpu.VMEM)
+    dma = pltpu.SemaphoreType.DMA
+    return pl.pallas_call(
+        functools.partial(moe_kernel, layer),
+        out_shape=jax.ShapeDtypeStruct((toks, d_model), BF16),
+        in_specs=[vmem] * 3 + [any_spec] * 6,
+        out_specs=vmem,
+        scratch_shapes=[
+            pltpu.VMEM((4, toks, d_model), BF16),
+            pltpu.VMEM((4, experts, toks), F32),
+            pltpu.VMEM((experts * ff, d_model), BF16),
+            pltpu.VMEM((experts * ff, d_model), BF16),
+            pltpu.VMEM((experts, ff, d_model), BF16),
+            pltpu.VMEM((experts, d_model, ff), BF16),
+            pltpu.VMEM((shared, d_model), BF16),
+            pltpu.VMEM((shared, d_model), BF16),
+            pltpu.VMEM((shared, d_model), BF16),
+            pltpu.VMEM((3, d_model, 2 * toks), F32),
+            pltpu.VMEM((3, d_model, toks), F32),
+            dma((6,)), dma((3,)), dma((3,)), dma((3,)), dma((3,)), dma((3,)), dma((3,)),
+        ],
+        compiler_params=pltpu.CompilerParams(
+            collective_id=layer, has_side_effects=True, vmem_limit_bytes=40 * 1024 * 1024),
+        name="expert_exchange",
+    )(x, g, route, w1, w3, w2, w1s, w3s, w2s)
 
 
 def solution(mesh):
-    group = mesh.shape['dp']
     tok_axes = ('replica', 'dp')
     in_specs = (
         P(tok_axes, None), P(tok_axes), P(None, tok_axes, None, None),
@@ -247,34 +379,18 @@
     )
 
     def device_step(x, lengths, cache, w_q, w_o, expert_ids, slots, route_w, w1_exp, w3_exp, w2_exp, w1_sh, w3_sh, w2_sh):
-        batch_dev, d_model = x.shape
-        local_experts = w1_exp.shape[1]
-        experts = local_experts * group
-        top_k = expert_ids.shape[2]
-        capacity = max(1, (2 * batch_dev * top_k) // experts)
-        resid = x
+        layers, local, d_model, ff = w1_exp.shape
         place, order, sorted_len = bucket_order(lengths)
         cache_t = jnp.swapaxes(cache, 2, 3)
-        for layer_idx in range(cache.shape[0]):
-            resid, ffn_in = attention(layer_idx, place, order, sorted_len, resid, cache_t, w_q, w_o)
-            gathered = lax.all_gather(ffn_in, 'dp', axis=0, tiled=True)
-            shared_h = gated_hidden(gathered, w1_sh[layer_idx], w3_sh[layer_idx])
-            shared_part = jnp.dot(shared_h, w2_sh[layer_idx], preferred_element_type=jnp.float32)
-            shared_out = lax.psum_scatter(shared_part, 'dp', scatter_dimension=0, tiled=True)
-            select = route_select(expert_ids[layer_idx], slots[layer_idx], experts, capacity)
-            dispatch = jnp.sum(select, axis=1)
-            send_buf = jnp.einsum('br,bd->rd', dispatch, ffn_in, preferred_element_type=jnp.float32).astype(jnp.bfloat16)
-            send_buf = send_buf.reshape(group, local_experts, capacity, d_model)
-            recv_buf = lax.all_to_all(send_buf, 'dp', 0, 0, tiled=True)
-            gate_in = jnp.einsum('sncd,ndf->nscf', recv_buf, w3_exp[layer_idx], preferred_element_type=jnp.float32)
-            up_in = jnp.einsum('sncd,ndf->nscf', recv_buf, w1_exp[layer_idx], preferred_element_type=jnp.float32)
-            hidden = (jax.nn.silu(gate_in) * up_in).astype(jnp.bfloat16)
-            expert_out = jnp.einsum('nscf,nfd->sncd', hidden, w2_exp[layer_idx], preferred_element_type=jnp.float32).astype(jnp.bfloat16)
-            returned = lax.all_to_all(expert_out, 'dp', 0, 0, tiled=True)
-            returned = returned.reshape(experts * capacity, d_model)
-            picked = jnp.einsum('cls,se->cle', select, returned, preferred_element_type=jnp.float32)
-            routed = jnp.sum(route_w[layer_idx][:, :, None] * picked, axis=1)
-            resid = (resid.astype(jnp.float32) + routed + shared_out).astype(jnp.bfloat16)
+        by_choice = [jnp.transpose(a, (2, 0, 1)) for a in (expert_ids, slots, route_w)]
+        w1 = jnp.swapaxes(w1_exp, 2, 3).reshape(layers, local * ff, d_model)
+        w3 = jnp.swapaxes(w3_exp, 2, 3).reshape(layers, local * ff, d_model)
+        w1s, w3s = jnp.swapaxes(w1_sh, 1, 2), jnp.swapaxes(w3_sh, 1, 2)
+        experts = local * mesh.shape['dp']
+        resid = x
+        for layer in range(layers):
+            resid, ffn_in, route = attention(layer, place, order, sorted_len, resid, cache_t, w_q, w_o, *by_choice, experts)
+            resid = moe(layer, resid, ffn_in, route, w1, w3, w2_exp, w1s, w3s, w2_sh)
         return resid
 
     return jax.shard_map(device_step, mesh=mesh, in_specs=in_specs, out_specs=P(tok_axes, None), check_vma=False)

time: 170 us -> 94.4 us (0.56)
  Pallas kernels: 52.9 us -> 85.5 us
  blocking collectives: 29.4 us -> 0 us
  waiting for transfers between devices: 27.7 us -> 0 us
  matrix products: 18.3 us -> 0 us
  starting transfers between devices: 14.7 us -> 0 us
  between operations: 13.7 us -> 0.2 us
  other arithmetic: 5.52 us -> 1.6 us
    pallas_call x0 -> x2, Pallas kernels: none -> 32.1 us  [moe(): pl.pallas_call(functools.partial(moe_kernel, layer), out_shape=jax.ShapeD...]
    all_gather x2 -> x0, blocking collectives: 29.4 us -> none  [device_step(): gathered = lax.all_gather(ffn_in, 'dp', axis=0, tiled=True)]
    all_to_all x4 -> x0, waiting for transfers between devices: 27.6 us -> none  [the longest x2 27.6 us: device_step(): returned = lax.all_to_all(expert_out, 'dp', 0, 0, tiled=True)]
    dot_general x12 -> x0, matrix products: 18.3 us -> none  [the longest x2 5.52 us: device_step(): jnp.einsum('nscf,nfd->sncd', hidden, w2_exp[layer_idx], preferred_element...]
    all_to_all x4 -> x0, starting transfers between devices: 14.7 us -> none  [the longest x2 7.7 us: device_step(): recv_buf = lax.all_to_all(send_buf, 'dp', 0, 0, tiled=True)]
    convert_element_type x2 -> x0, other arithmetic: 2.5 us -> none  [device_step(): (resid.astype(jnp.float32) + routed + shared_out).astype(jnp.bfloat16)]
    convert_element_type x2 -> x0, local copies, waits for them, and re-layouts: 1.89 us -> none  [device_step(): jnp.einsum('nscf,nfd->sncd', hidden, w2_exp[layer_idx], preferred_element...]
    unnamed x22 -> x35, local copies, waits for them, and re-layouts: 4.26 us -> 6.1 us
  transfers between devices with their start and end apart: 6 -> 0, of which waited for: 2 -> 0; matrix products, arithmetic and copies ran while one was open for 11% -> 0% of each run, Pallas kernels for 0% -> 0%
where the time goes in v2:
time: 94.4 us; the launch traced here: 93.4 us
  Pallas kernels  85.5 us (91%)
  local copies, waits for them, and re-layouts  6.1 us (6%)
  other arithmetic  1.6 us (2%)
    pallas_call x2, Pallas kernels, attention(): pl.pallas_call(functools.partial(attn_kernel, layer, slots), out_shape=(j...  53.4 us
    pallas_call x2, Pallas kernels, moe(): pl.pallas_call(functools.partial(moe_kernel, layer), out_shape=jax.ShapeD...  32.1 us
    unnamed x35, local copies, waits for them, and re-layouts  6.1 us

profile of v2, /device:TPU:0, one launch (start us, length us, event | category | flops | bytes accessed | tf_op | source)
XLA Modules:
  0.0 93.4 jit_solution(16420597008016552555)
XLA Ops:
  0.0 0.7 and_select_fusion
  0.7 0.2 convert_reduce_fusion
  0.8 0.8 select_reduce_fusion
  1.6 0.0 copy-start.3
  1.6 1.3 %copy-done.3 = bf16[2,256,1152]{2,1,0:T(8,128)(2,1)S(1)} copy-done((bf16[2,256,1152]{2,1,0:T(8,128)(2,1)S(1)}, bf16[2,256,1152]{2,1,0:T(8,128)(2,1)}, u32[]{:S(2)}) %copy-start.3) | copy-done | bytes 1179672
  2.9 1.2 %copy-done.5 = bf16[2,1024,256]{2,1,0:T(8,128)(2,1)S(1)} copy-done((bf16[2,1024,256]{2,1,0:T(8,128)(2,1)S(1)}, bf16[2,1024,256]{2,1,0:T(8,128)(2,1)}, u32[]{:S(2)}) %copy-start.5) | copy-done | bytes 1048600
  4.1 0.8 copy-done.10
  5.0 0.7 copy-done.11
  5.7 0.7 copy-done.13
  6.3 0.7 copy-done.15
  7.0 0.0 copy-start.8
  7.1 0.0 copy-start.9
  7.1 26.8 %latent_attention.2 = (bf16[128,256]{1,0:T(8,128)(2,1)S(1)}, bf16[128,256]{1,0:T(8,128)(2,1)S(1)}, f32[64,128]{1,0:T(8,128)S(1)}) custom-call(s32[128]{0:T(128)S(1)} %get-tuple-element.18.order_ref, s32[128]{0:T(128)S(1)} %get-tuple-element.17.slen_ref, s32[1,128]{1,0:T(1,128)S(1)} %bitcast.27, bf16[128,256]{1,0:T(8,128)(2,1)S(1)} %copy-done.10, ...), custom_call_target="tpu_custom_call" | custom-call | tf_op jit(solution)/shard_map/latent_attention/pallas_call | solution.py:216
  33.9 0.0 copy-done
  33.9 0.0 copy-done.1
  33.9 0.0 copy-done.2
  34.0 0.0 copy-done.7
  34.0 0.0 copy-done.8
  34.0 0.0 copy-start.4
  34.0 0.0 copy-start.6
  34.0 0.0 copy-start.12
  34.0 0.0 copy-start.14
  34.0 0.0 copy-start.16
  34.0 16.4 %expert_exchange.2.x_ref = bf16[128,256]{1,0:T(8,128)(2,1)S(1)} custom-call(bf16[128,256]{1,0:T(8,128)(2,1)S(1)} %get-tuple-element.11.x_ref, bf16[128,256]{1,0:T(8,128)(2,1)S(1)} %get-tuple-element.12.g_ref, f32[64,128]{1,0:T(8,128)S(1)} %get-tuple-element.13.route_ref, bf16[2,2816,256]{2,1,0:T(8,128)(2,1)S(1)} %bitcast.13, ...), custom_call_target="tpu_custom_call" | custom-call | tf_op jit(solution)/shard_map/expert_exchange/pallas_call | solution.py:346
  50.5 0.0 copy-done.4
  50.5 0.0 copy-done.6
  50.5 0.0 copy-done.12
  50.5 0.0 copy-done.14
  50.5 0.0 copy-done.16
  50.5 26.6 %latent_attention.3 = (bf16[128,256]{1,0:T(8,128)(2,1)S(1)}, bf16[128,256]{1,0:T(8,128)(2,1)S(1)}, f32[64,128]{1,0:T(8,128)S(1)}) custom-call(s32[128]{0:T(128)S(1)} %get-tuple-element.18.order_ref, s32[128]{0:T(128)S(1)} %get-tuple-element.17.slen_ref, s32[1,128]{1,0:T(1,128)S(1)} %bitcast.28, bf16[128,256]{1,0:T(8,128)(2,1)S(1)} %expert_exchange.2.x_ref, ...), custom_call_target="tpu_custom_call" | custom-call | tf_op jit(solution)/shard_map/latent_attention/pallas_call | solution.py:216
  77.1 15.6 %expert_exchange.3 = bf16[128,256]{1,0:T(8,128)(2,1)S(1)} custom-call(bf16[128,256]{1,0:T(8,128)(2,1)S(1)} %get-tuple-element.14.x_ref, bf16[128,256]{1,0:T(8,128)(2,1)S(1)} %get-tuple-element.15.g_ref, f32[64,128]{1,0:T(8,128)S(1)} %get-tuple-element.16.route_ref, bf16[2,2816,256]{2,1,0:T(8,128)(2,1)S(1)} %bitcast.14, bf16[2,2816,256]{2,1,0:T(8,128)(2,1)S(1)} %bitcast.16, ...), custom_call_target="tpu_custom_call" | custom-call | tf_op jit(solution)/shard_map/expert_exchange/pallas_call | solution.py:346
  92.7 0.6 copy.16
  (10 shorter events, 0.0 us)
Async XLA Ops:
  1.6 1.3 %copy-start.3 = (bf16[2,256,1152]{2,1,0:T(8,128)(2,1)S(1)}, bf16[2,256,1152]{2,1,0:T(8,128)(2,1)}, u32[]{:S(2)}) copy-start(bf16[2,256,1152]{2,1,0:T(8,128)(2,1)} %wq_hbm.3) | copy-start | bytes 3538948
  2.9 1.2 %copy-start.5 = (bf16[2,1024,256]{2,1,0:T(8,128)(2,1)S(1)}, bf16[2,1024,256]{2,1,0:T(8,128)(2,1)}, u32[]{:S(2)}) copy-start(bf16[2,1024,256]{2,1,0:T(8,128)(2,1)} %wo_hbm.3) | copy-start | bytes 3145732
  4.1 0.8 copy-start.10
  5.0 0.7 copy-start.11
  5.7 0.7 copy-start.13
  6.3 0.7 copy-start.15
  7.0 26.9 %copy-start = (bf16[2,16,256,176]{2,3,1,0:T(8,128)(2,1)S(1)}, bf16[2,16,256,176]{2,3,1,0:T(8,128)(2,1)}, u32[]{:S(2)}) copy-start(bf16[2,16,256,176]{2,3,1,0:T(8,128)(2,1)} %param.22) | copy-start | bytes 8650756
  7.0 26.9 %copy-start.1 = (bf16[2,16,256,176]{2,3,1,0:T(8,128)(2,1)S(1)}, bf16[2,16,256,176]{2,3,1,0:T(8,128)(2,1)}, u32[]{:S(2)}) copy-start(bf16[2,16,256,176]{2,3,1,0:T(8,128)(2,1)} %param.23) | copy-start | bytes 8650756
  7.0 26.9 %copy-start.2 = (bf16[2,16,176,256]{3,2,1,0:T(8,128)(2,1)S(1)}, bf16[2,16,176,256]{3,2,1,0:T(8,128)(2,1)}, u32[]{:S(2)}) copy-start(bf16[2,16,176,256]{3,2,1,0:T(8,128)(2,1)} %w2_hbm.3) | copy-start | bytes 8650756
  7.0 26.9 %copy-start.7 = (bf16[2,256,88]{1,2,0:T(8,128)(2,1)S(1)}, bf16[2,256,88]{1,2,0:T(8,128)(2,1)}, u32[]{:S(2)}) copy-start(bf16[2,256,88]{1,2,0:T(8,128)(2,1)} %param.25) | copy-start | bytes 270340
  7.0 26.9 %copy-start.8 = (bf16[2,256,88]{1,2,0:T(8,128)(2,1)S(1)}, bf16[2,256,88]{1,2,0:T(8,128)(2,1)}, u32[]{:S(2)}) copy-start(bf16[2,256,88]{1,2,0:T(8,128)(2,1)} %param.26) | copy-start | bytes 270340
  7.1 26.9 %copy-start.9 = (bf16[2,88,256]{2,1,0:T(8,128)(2,1)S(1)}, bf16[2,88,256]{2,1,0:T(8,128)(2,1)}, u32[]{:S(2)}) copy-start(bf16[2,88,256]{2,1,0:T(8,128)(2,1)} %w2s_hbm.3) | copy-start | bytes 270340
  34.0 16.5 %copy-start.4 = (bf16[2,256,1152]{2,1,0:T(8,128)(2,1)S(1)}, bf16[2,256,1152]{2,1,0:T(8,128)(2,1)}, u32[]{:S(2)}) copy-start(bf16[2,256,1152]{2,1,0:T(8,128)(2,1)} %wq_hbm.3) | copy-start | bytes 3538948
  34.0 16.5 %copy-start.6 = (bf16[2,1024,256]{2,1,0:T(8,128)(2,1)S(1)}, bf16[2,1024,256]{2,1,0:T(8,128)(2,1)}, u32[]{:S(2)}) copy-start(bf16[2,1024,256]{2,1,0:T(8,128)(2,1)} %wo_hbm.3) | copy-start | bytes 3145732
  34.0 16.5 %copy-start.12 = (s32[2,128,6]{1,0,2:T(2,128)S(1)}, s32[2,128,6]{1,0,2:T(2,128)}, u32[]{:S(2)}) copy-start(s32[2,128,6]{1,0,2:T(2,128)} %param.19) | copy-start | bytes 18436
  34.0 16.5 %copy-start.14 = (s32[2,128,6]{1,0,2:T(2,128)S(1)}, s32[2,128,6]{1,0,2:T(2,128)}, u32[]{:S(2)}) copy-start(s32[2,128,6]{1,0,2:T(2,128)} %param.20) | copy-start | bytes 18436
  34.0 16.5 %copy-start.16 = (f32[2,128,6]{1,0,2:T(2,128)S(1)}, f32[2,128,6]{1,0,2:T(2,128)}, u32[]{:S(2)}) copy-start(f32[2,128,6]{1,0,2:T(2,128)} %param.21) | copy-start | bytes 18436

commit v3 on v2

v3 whole, which is shorter than its diff:
```python
import functools
import jax
import jax.numpy as jnp
from jax import lax
from jax.experimental import pallas as pl
from jax.experimental.pallas import tpu as pltpu
from jax.sharding import PartitionSpec as P

NORM_EPS = 1e-6
ATT_SCALE = 1.0 / (192.0 ** 0.5)
LATENT = 512
CHUNK = 128
F32 = jnp.float32
BF16 = jnp.bfloat16


def rms_norm(values):
    vals32 = values.astype(F32)
    return vals32 * lax.rsqrt(jnp.mean(vals32 * vals32, axis=-1, keepdims=True) + NORM_EPS)


def bucket_order(lengths):
    count = lengths.shape[0]
    chunks = (lengths + (CHUNK - 1)) // CHUNK
    ids = jnp.arange(count, dtype=jnp.int32)
    ahead = (chunks[None, :] > chunks[:, None]) | ((chunks[None, :] == chunks[:, None]) & (ids[None, :] < ids[:, None]))
    place = jnp.sum(ahead.astype(jnp.int32), axis=1)
    hit = place[None, :] == ids[:, None]
    order = jnp.sum(jnp.where(hit, ids[None, :], 0), axis=1)
    sorted_len = jnp.sum(jnp.where(hit, lengths[None, :], 0), axis=1)
    return place, order, sorted_len


def attn_kernel(layer, slots, order_ref, slen_ref, place_ref, x_in, cache_ref, wq_hbm, wo_hbm,
                x_out, g_out, wq, wo, buf, qbd, obuf, pbuf, sem, wsem, xbuf):
    toks, d_model = x_in.shape
    kv_dim, seq_len = cache_ref.shape[2], cache_ref.shape[3]
    groups = toks // 8
    max_n = seq_len // CHUNK

    def group_n(g):
        return lax.div(slen_ref[g * 8] + (CHUNK - 1), CHUNK)

    def start_group(g):
        slot = lax.rem(g, slots)
        n = group_n(g)
        for k in range(max_n):
            @pl.when(k < n)
            def _():
                for i in range(8):
                    b = order_ref[g * 8 + i]
                    pltpu.make_async_copy(
                        cache_ref.at[layer, b, :, pl.ds(k * CHUNK, CHUNK)],
                        buf.at[slot, i // 4, k, pl.ds((i % 4) * kv_dim, kv_dim)], sem.at[slot]).start()

    wq_copy = pltpu.make_async_copy(wq_hbm.at[layer], wq, wsem.at[0])
    wo_copy = pltpu.make_async_copy(wo_hbm.at[layer], wo, wsem.at[1])
    wq_copy.start()
    x_copy = pltpu.make_async_copy(x_in, xbuf, wsem.at[2])
    if layer == 0:
        x_copy.start()
    x_ref = xbuf if layer == 0 else x_in
    lax.fori_loop(0, slots, lambda g, c: (start_group(g), c)[1], 0)
    wo_copy.start()

    rows = 2 * toks
    row_id = lax.broadcasted_iota(jnp.int32, (rows, toks), 0)
    place = place_ref[...]
    base = lax.shift_right_logical(place, 2) * 8 + lax.rem(place, 4)
    pick0 = (row_id == base).astype(BF16)
    pick1 = (row_id == base + 4).astype(BF16)
    if layer == 0:
        x_copy.wait()
    h = rms_norm(x_ref[...]).astype(BF16)
    wq_copy.wait()
    q = jnp.dot(h, wq[...], preferred_element_type=F32).astype(BF16)
    qrows = (jnp.dot(pick0, q[:, :kv_dim], preferred_element_type=F32)
             + jnp.dot(pick1, q[:, kv_dim:], preferred_element_type=F32))
    sub = lax.rem(lax.broadcasted_iota(jnp.int32, (rows, 1), 0), 4)
    twice = jnp.concatenate([qrows, qrows], axis=1)
    second = (lax.broadcasted_iota(jnp.int32, (rows, 2 * kv_dim), 1) >= kv_dim).astype(jnp.int32)
    for jj in range(2):
        lhs = jnp.where(sub == 2 * jj + second, twice, 0.0).astype(BF16)
        for t in range(2 * kv_dim // CHUNK):
            qbd[jj * (2 * kv_dim // CHUNK) + t] = lhs[:, t * CHUNK:(t + 1) * CHUNK]

    row16 = lax.broadcasted_iota(jnp.int32, (16, CHUNK), 0)
    sub16 = lax.rem(row16, 4)
    lane16 = lax.broadcasted_iota(jnp.int32, (16, CHUNK), 1)
    half16 = (row16 >= 8).astype(jnp.int32)
    seq16 = half16 * 4 + sub16

    def scores(g, nn):
        slot = lax.rem(g, slots)
        at16 = pl.ds(pl.multiple_of(g * 16, 16), 16)
        lhs = jnp.concatenate([qbd[t, at16, :] for t in range(qbd.shape[0])], axis=1)
        lens = jnp.zeros((16, CHUNK), jnp.int32)
        for i in range(8):
            lens = jnp.where(seq16 == i, slen_ref[g * 8 + i], lens)
        out = []
        for k in range(nn):
            rhs = jnp.concatenate([buf[slot, 0, k], buf[slot, 1, k]], axis=1)
            raw = jnp.dot(lhs, rhs, preferred_element_type=F32)
            s = jnp.concatenate([raw[0:8, :CHUNK], raw[8:16, CHUNK:]], axis=0) * ATT_SCALE
            out.append(jnp.where(lane16 + k * CHUNK < lens, s, -jnp.inf))
        return out

    def softmax(s):
        m = s[0]
        for t in s[1:]:
            m = jnp.maximum(m, t)
        m = jnp.max(m, axis=1, keepdims=True)
        e = [jnp.exp(t - m) for t in s]
        tot = e[0]
        for t in e[1:]:
            tot = tot + t
        inv = 1.0 / jnp.sum(tot, axis=1, keepdims=True)
        return [(t * inv) for t in e]

    def values(g, p):
        slot = lax.rem(g, slots)
        lhs, rhs = [], []
        for k, t in enumerate(p):
            for j in range(4):
                for half in range(2):
                    keep = (sub16 == j) & (half16 == half)
                    lhs.append(jnp.where(keep, t, 0.0).astype(BF16))
                    rhs.append(buf[slot, half, k, pl.ds(j * kv_dim, LATENT)])
        o = lax.dot_general(jnp.concatenate(lhs, axis=1), jnp.concatenate(rhs, axis=1),
                            (((1,), (1,)), ((), ())), preferred_element_type=F32)
        obuf[pl.ds(pl.multiple_of(g * 16, 16), 16), :] = o.astype(BF16)

    def wait_group(g, nn):
        slot = lax.rem(g, slots)
        view = buf.at[slot, :, pl.ds(0, nn)]
        pltpu.make_async_copy(view, view, sem.at[slot]).wait()

    def put_scores(g, nn):
        for k, t in enumerate(scores(g, nn)):
            pbuf[lax.rem(g, 2), k] = t

    def put_values(g, nn):
        values(g, softmax([pbuf[lax.rem(g, 2), k] for k in range(nn)]))

    def each_n(n, fn):
        for nn in range(1, max_n + 1):
            pl.when(n == nn)(functools.partial(fn, nn))

    def first(nn):
        wait_group(0, nn)
    each_n(group_n(0), first)
    put_scores(0, max_n)

    def body(g, _):
        each_n(group_n(g), functools.partial(wait_group, g))

        def both(nn):
            raw_prev = [pbuf[lax.rem(g - 1, 2), k] for k in range(nn)]
            s = scores(g, nn)
            values(g - 1, softmax(raw_prev))
            for k, t in enumerate(s):
                pbuf[lax.rem(g, 2), k] = t
        each_n(group_n(g - 1), both)

        @pl.when(g - 1 + slots < groups)
        def _():
            start_group(g - 1 + slots)
        return 0

    lax.fori_loop(1, groups, body, 0)
    each_n(group_n(groups - 1), functools.partial(put_values, groups - 1))

    wo_copy.wait()
    picked = obuf[...]
    total = x_ref[...].astype(F32)
    for head, pick in enumerate((pick0, pick1)):
        o = lax.dot_general(pick, picked, (((0,), (0,)), ((), ())), preferred_element_type=F32).astype(BF16)
        total = total + jnp.dot(o, wo[head * LATENT:(head + 1) * LATENT, :], preferred_element_type=F32)
    x_new = total.astype(BF16)
    x_out[...] = x_new
    g_out[...] = rms_norm(x_new).astype(BF16)


def attention(layer, place, order, sorted_len, x, cache_t, w_q, w_o, slots=8):
    toks, d_model = x.shape
    kv_dim, seq_len = cache_t.shape[2], cache_t.shape[3]
    any_spec = pl.BlockSpec(memory_space=pltpu.HBM)
    if layer == 0:
        x, w_q, w_o = (pltpu.with_memory_space_constraint(a, pltpu.HBM) for a in (x, w_q, w_o))
    smem = pl.BlockSpec(memory_space=pltpu.SMEM)
    vmem = pl.BlockSpec(memory_space=pltpu.VMEM)
    return pl.pallas_call(
        functools.partial(attn_kernel, layer, slots),
        out_shape=(jax.ShapeDtypeStruct((toks, d_model), BF16), jax.ShapeDtypeStruct((toks, d_model), BF16)),
        in_specs=[smem, smem, vmem, any_spec if layer == 0 else vmem, any_spec, any_spec, any_spec],
        out_specs=(vmem, vmem),
        scratch_shapes=[
            pltpu.VMEM(w_q.shape[1:], BF16),
            pltpu.VMEM(w_o.shape[1:], BF16),
            pltpu.VMEM((slots, 2, seq_len // CHUNK, 4 * kv_dim, CHUNK), BF16),
            pltpu.VMEM((4 * kv_dim // CHUNK, 2 * toks, CHUNK), BF16),
            pltpu.VMEM((2 * toks, LATENT), BF16),
            pltpu.VMEM((2, seq_len // CHUNK, 16, CHUNK), F32),
            pltpu.SemaphoreType.DMA((slots,)),
            pltpu.SemaphoreType.DMA((3,)),
            pltpu.VMEM((toks, d_model), BF16),
        ],
        compiler_params=pltpu.CompilerParams(vmem_limit_bytes=48 * 1024 * 1024),
        name="latent_attention",
    )(order, sorted_len, place.reshape(1, toks), x, cache_t, w_q, w_o)


MESH_ID = pl.DeviceIdType.MESH
EXP_STEP = 4


def moe_kernel(layer, x_ref, g_ref, ids_ref, slot_ref, gate_ref, w1, w3, w2, w1s, w3s, w2s, out_ref,
               gall, wall, route_ref, w2t, acc, part, gsend, grecv, rsend, rrecv, psend, precv):
    me = lax.axis_index('dp')
    core = lax.rem(me, 2)
    chip = lax.div(me, 2)
    partner = chip * 2 + (1 - core)
    cross = (1 - chip) * 2 + (1 - core)
    same = (1 - chip) * 2 + core
    peers = (partner, cross, same)
    _, experts, ff, d_model = w2.shape
    toks = x_ref.shape[0]

    expert_id = lax.broadcasted_iota(jnp.int32, route_ref.shape, 0)
    route = jnp.zeros(route_ref.shape, F32)
    for j in range(ids_ref.shape[0]):
        hit = (ids_ref[j, layer:layer + 1, :] == expert_id) & (slot_ref[j, layer:layer + 1, :] >= 0)
        route = route + jnp.where(hit, gate_ref[j, layer:layer + 1, :], 0.0)
    route_ref[...] = route

    barrier = pltpu.get_barrier_semaphore()
    for p in peers:
        pl.semaphore_signal(barrier, inc=1, device_id={'dp': p}, device_id_type=MESH_ID)
    pl.semaphore_wait(barrier, 3)

    gcopies, rcopies = [], []
    for i, p in enumerate(peers):
        rcopies.append(pltpu.make_async_remote_copy(
            route_ref.at[pl.ds(p * experts, experts)], wall.at[i + 1], rsend.at[i], rrecv.at[i],
            device_id={'dp': p}, device_id_type=MESH_ID))
        gcopies.append(pltpu.make_async_remote_copy(
            g_ref, gall.at[i + 1], gsend.at[i], grecv.at[i], device_id={'dp': p}, device_id_type=MESH_ID))
    for i in range(3):
        rcopies[i].start()
        gcopies[i].start()

    gall[0] = g_ref[...]
    wall[0] = route_ref[pl.ds(pl.multiple_of(me * experts, experts), experts), :]

    def flip(e, carry):
        w2t[e] = w2[layer, e].T
        return carry
    lax.fori_loop(0, experts, flip, 0)
    w2st = w2s[layer].T

    def gated(w3_rows, w1_rows, tok):
        dims = (((1,), (1,)), ((), ()))
        gate = lax.dot_general(w3_rows, tok, dims, preferred_element_type=F32)
        up = lax.dot_general(w1_rows, tok, dims, preferred_element_type=F32)
        return (gate * (1.0 / (1.0 + jnp.exp(-gate))) * up).astype(BF16)

    def ffn(blocks):
        tok = jnp.concatenate([gall[b] for b in blocks], axis=0)
        first = jnp.dot(w2st, gated(w3s[layer], w1s[layer], tok), preferred_element_type=F32)
        for n, b in enumerate(blocks):
            acc[b] = first[:, n * toks:(n + 1) * toks]

        def step(s, carry):
            rows = slice(s * EXP_STEP * ff, (s + 1) * EXP_STEP * ff)
            hid = gated(w3[layer, rows, :], w1[layer, rows, :], tok)
            total = [acc[b] for b in blocks]
            for i in range(EXP_STEP):
                e = s * EXP_STEP + i
                u = jnp.dot(w2t[e], hid[i * ff:(i + 1) * ff], preferred_element_type=F32)
                u = u.astype(BF16).astype(F32)
                for n, b in enumerate(blocks):
                    w = wall[b, e:e + 1, :]
                    total[n] = total[n] + jnp.where(w > 0.0, u[:, n * toks:(n + 1) * toks] * w, 0.0)
            for n, b in enumerate(blocks):
                acc[b] = total[n]
            return carry
        for s in range(experts // EXP_STEP):
            step(s, 0)

    def send_part(i, src, dst_ref, dst):
        return pltpu.make_async_remote_copy(
            src, dst_ref, psend.at[i], precv.at[i], device_id={'dp': dst}, device_id_type=MESH_ID)

    rcopies[0].wait_recv()
    gcopies[0].wait_recv()
    ffn((0, 1))
    home = send_part(0, acc.at[1], part.at[0], partner)
    home.start()

    rcopies[1].wait_recv()
    gcopies[1].wait_recv()
    ffn((2,))
    relay = send_part(1, acc.at[2], part.at[1], partner)
    relay.start()

    rcopies[2].wait_recv()
    gcopies[2].wait_recv()
    ffn((3,))
    relay.wait_recv()
    half = d_model // 2
    far = []
    for i in range(2):
        rows = slice(i * half, (i + 1) * half)
        acc[4, rows] = acc[3, rows] + part[1, rows]
        at = pl.ds(i * half, half)
        far.append(send_part(2 + i, acc.at[4, at], part.at[2, at], same))
        far[i].start()
    home.wait_recv()
    acc[0] = acc[0] + part[0]
    for i in range(2):
        rows = slice(i * half, (i + 1) * half)
        far[i].wait_recv()
        out_ref[:, rows] = (x_ref[:, rows].astype(F32) + (acc[0, rows] + part[2, rows]).T).astype(BF16)

    for c in gcopies + rcopies + [home, relay] + far:
        c.wait_send()


def moe(layer, x, g, ids, slot, gate, total_experts, w1, w3, w2, w1s, w3s, w2s):
    toks, d_model = x.shape
    _, experts, ff, _ = w2.shape
    vmem = pl.BlockSpec(memory_space=pltpu.VMEM)
    dma = pltpu.SemaphoreType.DMA
    return pl.pallas_call(
        functools.partial(moe_kernel, layer),
        out_shape=jax.ShapeDtypeStruct((toks, d_model), BF16),
        in_specs=[vmem] * 11,
        out_specs=vmem,
        scratch_shapes=[
            pltpu.VMEM((4, toks, d_model), BF16),
            pltpu.VMEM((4, experts, toks), F32),
            pltpu.VMEM((total_experts, toks), F32),
            pltpu.VMEM((experts, d_model, ff), BF16),
            pltpu.VMEM((5, d_model, toks), F32),
            pltpu.VMEM((3, d_model, toks), F32),
            dma((3,)), dma((3,)), dma((3,)), dma((3,)), dma((4,)), dma((4,)),
        ],
        compiler_params=pltpu.CompilerParams(
            collective_id=layer, has_side_effects=True, vmem_limit_bytes=40 * 1024 * 1024),
        name="expert_exchange",
    )(x, g, ids, slot, gate, w1, w3, w2, w1s, w3s, w2s)


def solution(mesh):
    tok_axes = ('replica', 'dp')
    in_specs = (
        P(tok_axes, None), P(tok_axes), P(None, tok_axes, None, None),
        P(None, None, None), P(None, None, None),
        P(None, tok_axes, None), P(None, tok_axes, None), P(None, tok_axes, None),
        P(None, 'dp', None, None), P(None, 'dp', None, None), P(None, 'dp', None, None),
        P(None, None, 'dp'), P(None, None, 'dp'), P(None, 'dp', None),
    )

    def device_step(x, lengths, cache, w_q, w_o, expert_ids, slots, route_w, w1_exp, w3_exp, w2_exp, w1_sh, w3_sh, w2_sh):
        layers, local, d_model, ff = w1_exp.shape
        place, order, sorted_len = bucket_order(lengths)
        cache_t = jnp.swapaxes(cache, 2, 3)
        by_choice = [jnp.transpose(a, (2, 0, 1)) for a in (expert_ids, slots, route_w)]
        w1 = jnp.swapaxes(w1_exp, 2, 3).reshape(layers, local * ff, d_model)
        w3 = jnp.swapaxes(w3_exp, 2, 3).reshape(layers, local * ff, d_model)
        w1s, w3s = jnp.swapaxes(w1_sh, 1, 2), jnp.swapaxes(w3_sh, 1, 2)
        experts = local * mesh.shape['dp']
        resid = x
        for layer in range(layers):
            resid, ffn_in = attention(layer, place, order, sorted_len, resid, cache_t, w_q, w_o)
            resid = moe(layer, resid, ffn_in, *by_choice, experts, w1, w3, w2_exp, w1s, w3s, w2_sh)
        return resid

    return jax.shard_map(device_step, mesh=mesh, in_specs=in_specs, out_specs=P(tok_axes, None), check_vma=False)
```

time: 94.4 us -> 84.2 us (0.89)
  local copies, waits for them, and re-layouts: 6.1 us -> 0.7 us
  Pallas kernels: 85.5 us -> 81.4 us
    unnamed x35 -> x23, local copies, waits for them, and re-layouts: 6.1 us -> 0.7 us
    pallas_call x2, Pallas kernels: 32.1 us -> 28.9 us  [moe(): pl.pallas_call(functools.partial(moe_kernel, layer), out_shape=jax.ShapeD...]
where the time goes in v3:
time: 84.2 us; the launch traced here: 84 us
  Pallas kernels  81.4 us (97%)
  other arithmetic  1.6 us (2%)
    pallas_call x2, Pallas kernels, attention(): pl.pallas_call(functools.partial(attn_kernel, layer, slots), out_shape=(j...  52.5 us
    pallas_call x2, Pallas kernels, moe(): pl.pallas_call(functools.partial(moe_kernel, layer), out_shape=jax.ShapeD...  28.9 us

profile of v3, /device:TPU:0, one launch (start us, length us, event | category | flops | bytes accessed | tf_op | source)
XLA Modules:
  0.0 84.0 jit_solution(7790456368768703228)
XLA Ops:
  0.0 0.7 and_select_fusion
  0.7 0.2 convert_reduce_fusion
  0.8 0.8 select_reduce_fusion
  1.6 0.0 copy-start
  1.6 0.0 copy-start.1
  1.6 0.0 copy-start.2
  1.6 0.0 copy-start.5
  1.7 0.0 copy-start.6
  1.7 0.0 copy-start.7
  1.7 0.0 copy-start.8
  1.7 0.0 copy-start.9
  1.7 0.0 copy-start.10
  1.7 26.3 %latent_attention.2 = (bf16[128,256]{1,0:T(8,128)(2,1)S(1)}, bf16[128,256]{1,0:T(8,128)(2,1)S(1)}) custom-call(s32[128]{0:T(128)S(1)} %get-tuple-element.14.order_ref, s32[128]{0:T(128)S(1)} %get-tuple-element.13.slen_ref, s32[1,128]{1,0:T(1,128)S(1)} %bitcast.27, bf16[128,256]{1,0:T(8,128)(2,1)} %x_in.1, bf16[2,128,576,512]{3,2,1,0:T(8,128)(2,1)} %bitcast.1.cache_ref, ...), custom_call_target="tpu_custom_call" | custom-call | tf_op jit(solution)/shard_map/latent_attention/pallas_call | solution.py:192
  28.1 0.0 copy-done
  28.1 0.0 copy-done.1
  28.1 0.0 copy-done.2
  28.1 0.0 copy-done.5
  28.1 0.0 copy-done.6
  28.1 0.0 copy-done.7
  28.1 0.0 copy-done.8
  28.1 0.0 copy-done.9
  28.1 0.0 copy-done.10
  28.2 0.0 copy-start.3
  28.2 0.0 copy-start.4
  28.2 15.5 %expert_exchange.2.x_in = bf16[128,256]{1,0:T(8,128)(2,1)S(1)} custom-call(bf16[128,256]{1,0:T(8,128)(2,1)S(1)} %get-tuple-element.9.x_ref, bf16[128,256]{1,0:T(8,128)(2,1)S(1)} %get-tuple-element.10.g_ref, s32[6,2,128]{2,1,0:T(2,128)S(1)} %bitcast.21, s32[6,2,128]{2,1,0:T(2,128)S(1)} %bitcast.23, f32[6,2,128]{2,1,0:T(2,128)S(1)} %bitcast.25, ...), custom_call_target="tpu_custom_call" | custom-call | tf_op jit(solution)/shard_map/expert_exchange/pallas_call | solution.py:334
  43.7 0.0 copy-done.3
  43.7 0.0 copy-done.4
  43.7 26.2 %latent_attention.3 = (bf16[128,256]{1,0:T(8,128)(2,1)S(1)}, bf16[128,256]{1,0:T(8,128)(2,1)S(1)}) custom-call(s32[128]{0:T(128)S(1)} %get-tuple-element.14.order_ref, s32[128]{0:T(128)S(1)} %get-tuple-element.13.slen_ref, s32[1,128]{1,0:T(1,128)S(1)} %bitcast.28, bf16[128,256]{1,0:T(8,128)(2,1)S(1)} %expert_exchange.2.x_in, ...), custom_call_target="tpu_custom_call" | custom-call | tf_op jit(solution)/shard_map/latent_attention/pallas_call | solution.py:192
  69.9 13.4 %expert_exchange.3 = bf16[128,256]{1,0:T(8,128)(2,1)S(1)} custom-call(bf16[128,256]{1,0:T(8,128)(2,1)S(1)} %get-tuple-element.11.x_ref, bf16[128,256]{1,0:T(8,128)(2,1)S(1)} %get-tuple-element.12.g_ref, s32[6,2,128]{2,1,0:T(2,128)S(1)} %bitcast.22, s32[6,2,128]{2,1,0:T(2,128)S(1)} %bitcast.24, f32[6,2,128]{2,1,0:T(2,128)S(1)} %bitcast.26, ...), custom_call_target="tpu_custom_call" | custom-call | tf_op jit(solution)/shard_map/expert_exchange/pallas_call | solution.py:334
  83.3 0.6 copy.16
Async XLA Ops:
  1.6 26.5 %copy-start = (bf16[2,16,256,176]{2,3,1,0:T(8,128)(2,1)S(1)}, bf16[2,16,256,176]{2,3,1,0:T(8,128)(2,1)}, u32[]{:S(2)}) copy-start(bf16[2,16,256,176]{2,3,1,0:T(8,128)(2,1)} %param.22) | copy-start | bytes 8650756
  1.6 26.5 %copy-start.1 = (bf16[2,16,256,176]{2,3,1,0:T(8,128)(2,1)S(1)}, bf16[2,16,256,176]{2,3,1,0:T(8,128)(2,1)}, u32[]{:S(2)}) copy-start(bf16[2,16,256,176]{2,3,1,0:T(8,128)(2,1)} %param.23) | copy-start | bytes 8650756
  1.6 26.4 %copy-start.2 = (bf16[2,16,176,256]{3,2,1,0:T(8,128)(2,1)S(1)}, bf16[2,16,176,256]{3,2,1,0:T(8,128)(2,1)}, u32[]{:S(2)}) copy-start(bf16[2,16,176,256]{3,2,1,0:T(8,128)(2,1)} %w2.3) | copy-start | bytes 8650756
  1.6 26.4 %copy-start.5 = (bf16[2,256,88]{1,2,0:T(8,128)(2,1)S(1)}, bf16[2,256,88]{1,2,0:T(8,128)(2,1)}, u32[]{:S(2)}) copy-start(bf16[2,256,88]{1,2,0:T(8,128)(2,1)} %param.25) | copy-start | bytes 270340
  1.7 26.4 %copy-start.6 = (bf16[2,256,88]{1,2,0:T(8,128)(2,1)S(1)}, bf16[2,256,88]{1,2,0:T(8,128)(2,1)}, u32[]{:S(2)}) copy-start(bf16[2,256,88]{1,2,0:T(8,128)(2,1)} %param.26) | copy-start | bytes 270340
  1.7 26.4 %copy-start.7 = (bf16[2,88,256]{2,1,0:T(8,128)(2,1)S(1)}, bf16[2,88,256]{2,1,0:T(8,128)(2,1)}, u32[]{:S(2)}) copy-start(bf16[2,88,256]{2,1,0:T(8,128)(2,1)} %w2s.3) | copy-start | bytes 270340
  1.7 26.4 %copy-start.8 = (s32[2,128,6]{1,0,2:T(2,128)S(1)}, s32[2,128,6]{1,0,2:T(2,128)}, u32[]{:S(2)}) copy-start(s32[2,128,6]{1,0,2:T(2,128)} %param.19) | copy-start | bytes 18436
  1.7 26.4 %copy-start.9 = (s32[2,128,6]{1,0,2:T(2,128)S(1)}, s32[2,128,6]{1,0,2:T(2,128)}, u32[]{:S(2)}) copy-start(s32[2,128,6]{1,0,2:T(2,128)} %param.20) | copy-start | bytes 18436
  1.7 26.4 %copy-start.10 = (f32[2,128,6]{1,0,2:T(2,128)S(1)}, f32[2,128,6]{1,0,2:T(2,128)}, u32[]{:S(2)}) copy-start(f32[2,128,6]{1,0,2:T(2,128)} %param.21) | copy-start | bytes 18436
  28.2 15.5 %copy-start.3 = (bf16[2,256,1152]{2,1,0:T(8,128)(2,1)S(1)}, bf16[2,256,1152]{2,1,0:T(8,128)(2,1)}, u32[]{:S(2)}) copy-start(bf16[2,256,1152]{2,1,0:T(8,128)(2,1)} %wq_hbm.3) | copy-start | bytes 3538948
  28.2 15.5 %copy-start.4 = (bf16[2,1024,256]{2,1,0:T(8,128)(2,1)S(1)}, bf16[2,1024,256]{2,1,0:T(8,128)(2,1)}, u32[]{:S(2)}) copy-start(bf16[2,1024,256]{2,1,0:T(8,128)(2,1)} %wo_hbm.3) | copy-start | bytes 3145732

commit v4 on v3

--- a/solution.py
+++ b/solution.py
@@ -11,6 +11,8 @@
 LATENT = 512
 CHUNK = 128
 F32 = jnp.float32
+MXU_COLS = 256
+VBLK = 64
 BF16 = jnp.bfloat16
 
 
@@ -44,14 +46,15 @@
     def start_group(g):
         slot = lax.rem(g, slots)
         n = group_n(g)
-        for k in range(max_n):
-            @pl.when(k < n)
+        for nn in range(1, max_n + 1):
+            @pl.when(n == nn)
             def _():
+                cols = pl.ds(0, nn * CHUNK)
                 for i in range(8):
                     b = order_ref[g * 8 + i]
                     pltpu.make_async_copy(
-                        cache_ref.at[layer, b, :, pl.ds(k * CHUNK, CHUNK)],
-                        buf.at[slot, i // 4, k, pl.ds((i % 4) * kv_dim, kv_dim)], sem.at[slot]).start()
+                        cache_ref.at[layer, b, :, cols],
+                        buf.at[slot, i // 4, pl.ds((i % 4) * kv_dim, kv_dim), cols], sem.at[slot]).start()
 
     wq_copy = pltpu.make_async_copy(wq_hbm.at[layer], wq, wsem.at[0])
     wo_copy = pltpu.make_async_copy(wo_hbm.at[layer], wo, wsem.at[1])
@@ -99,7 +102,8 @@
             lens = jnp.where(seq16 == i, slen_ref[g * 8 + i], lens)
         out = []
         for k in range(nn):
-            rhs = jnp.concatenate([buf[slot, 0, k], buf[slot, 1, k]], axis=1)
+            cols = pl.ds(k * CHUNK, CHUNK)
+            rhs = jnp.concatenate([buf[slot, 0, :, cols], buf[slot, 1, :, cols]], axis=1)
             raw = jnp.dot(lhs, rhs, preferred_element_type=F32)
             s = jnp.concatenate([raw[0:8, :CHUNK], raw[8:16, CHUNK:]], axis=0) * ATT_SCALE
             out.append(jnp.where(lane16 + k * CHUNK < lens, s, -jnp.inf))
@@ -117,22 +121,42 @@
         inv = 1.0 / jnp.sum(tot, axis=1, keepdims=True)
         return [(t * inv) for t in e]
 
+    lane_blk = lax.broadcasted_iota(jnp.int32, (VBLK, CHUNK), 1)
+
     def values(g, p):
         slot = lax.rem(g, slots)
+        at16 = pl.ds(pl.multiple_of(g * 16, 16), 16)
         lhs, rhs = [], []
         for k, t in enumerate(p):
             for j in range(4):
                 for half in range(2):
                     keep = (sub16 == j) & (half16 == half)
                     lhs.append(jnp.where(keep, t, 0.0).astype(BF16))
-                    rhs.append(buf[slot, half, k, pl.ds(j * kv_dim, LATENT)])
+                    rhs.append(buf[slot, half, pl.ds(j * kv_dim, MXU_COLS), pl.ds(k * CHUNK, CHUNK)])
         o = lax.dot_general(jnp.concatenate(lhs, axis=1), jnp.concatenate(rhs, axis=1),
                             (((1,), (1,)), ((), ())), preferred_element_type=F32)
-        obuf[pl.ds(pl.multiple_of(g * 16, 16), 16), :] = o.astype(BF16)
+        obuf[at16, :MXU_COLS] = o.astype(BF16)
+        rounded = [t.astype(BF16).astype(F32) for t in p]
+        blocks = (LATENT - MXU_COLS) // VBLK
+        picked = [jnp.zeros((VBLK, CHUNK), F32) for _ in range(blocks)]
+        for half in range(2):
+            for j in range(4):
+                for c in range(blocks):
+                    sums = [None, None]
+                    for k in range(len(p)):
+                        tile = buf[slot, half, pl.ds(j * kv_dim + MXU_COLS + c * VBLK, VBLK), pl.ds(k * CHUNK, CHUNK)].astype(F32)
+                        for head in range(2):
+                            row = half * 8 + head * 4 + j
+                            term = tile * rounded[k][row:row + 1, :]
+                            sums[head] = term if k == 0 else sums[head] + term
+                    for head in range(2):
+                        row = half * 8 + head * 4 + j
+                        picked[c] = jnp.where(lane_blk == row, jnp.sum(sums[head], axis=1, keepdims=True), picked[c])
+        obuf[at16, MXU_COLS:] = jnp.concatenate(picked, axis=0).T[:16].astype(BF16)
 
     def wait_group(g, nn):
         slot = lax.rem(g, slots)
-        view = buf.at[slot, :, pl.ds(0, nn)]
+        view = buf.at[slot, :, :, pl.ds(0, nn * CHUNK)]
         pltpu.make_async_copy(view, view, sem.at[slot]).wait()
 
     def put_scores(g, nn):
@@ -197,7 +221,7 @@
         scratch_shapes=[
             pltpu.VMEM(w_q.shape[1:], BF16),
             pltpu.VMEM(w_o.shape[1:], BF16),
-            pltpu.VMEM((slots, 2, seq_len // CHUNK, 4 * kv_dim, CHUNK), BF16),
+            pltpu.VMEM((slots, 2, 4 * kv_dim, seq_len), BF16),
             pltpu.VMEM((4 * kv_dim // CHUNK, 2 * toks, CHUNK), BF16),
             pltpu.VMEM((2 * toks, LATENT), BF16),
             pltpu.VMEM((2, seq_len // CHUNK, 16, CHUNK), F32),

time: 84.2 us -> 77.6 us (0.922)
  Pallas kernels: 81.4 us -> 75 us
    pallas_call x2, Pallas kernels: 52.5 us -> 45.7 us  [attention(): pl.pallas_call(functools.partial(attn_kernel, layer, slots), out_shape=(j...]
where the time goes in v4:
time: 77.6 us
  Pallas kernels  75 us (97%)
  other arithmetic  1.6 us (2%)
    pallas_call x2, Pallas kernels, attention(): pl.pallas_call(functools.partial(attn_kernel, layer, slots), out_shape=(j...  45.7 us
    pallas_call x2, Pallas kernels, moe(): pl.pallas_call(functools.partial(moe_kernel, layer), out_shape=jax.ShapeD...  29.3 us

profile of v4, /device:TPU:0, one launch (start us, length us, event | category | flops | bytes accessed | tf_op | source)
XLA Modules:
  0.0 77.6 jit_solution(9365813266678406574)
XLA Ops:
  0.0 0.7 and_select_fusion
  0.7 0.2 convert_reduce_fusion
  0.8 0.8 select_reduce_fusion
  1.6 0.0 copy-start
  1.6 0.0 copy-start.1
  1.6 0.0 copy-start.2
  1.6 0.0 copy-start.5
  1.7 0.0 copy-start.6
  1.7 0.0 copy-start.7
  1.7 0.0 copy-start.8
  1.7 0.0 copy-start.9
  1.7 0.0 copy-start.10
  1.7 22.9 %latent_attention.2 = (bf16[128,256]{1,0:T(8,128)(2,1)S(1)}, bf16[128,256]{1,0:T(8,128)(2,1)S(1)}) custom-call(s32[128]{0:T(128)S(1)} %get-tuple-element.14.order_ref, s32[128]{0:T(128)S(1)} %get-tuple-element.13.slen_ref, s32[1,128]{1,0:T(1,128)S(1)} %bitcast.27, bf16[128,256]{1,0:T(8,128)(2,1)} %x_in.1, bf16[2,128,576,512]{3,2,1,0:T(8,128)(2,1)} %bitcast.1.cache_ref, ...), custom_call_target="tpu_custom_call" | custom-call | tf_op jit(solution)/shard_map/latent_attention/pallas_call | solution.py:216
  24.7 0.0 copy-done
  24.7 0.0 copy-done.1
  24.7 0.0 copy-done.2
  24.7 0.0 copy-done.5
  24.7 0.0 copy-done.6
  24.7 0.0 copy-done.7
  24.7 0.0 copy-done.8
  24.7 0.0 copy-done.9
  24.7 0.0 copy-done.10
  24.7 0.0 copy-start.3
  24.8 0.0 copy-start.4
  24.8 15.9 %expert_exchange.2.x_in = bf16[128,256]{1,0:T(8,128)(2,1)S(1)} custom-call(bf16[128,256]{1,0:T(8,128)(2,1)S(1)} %get-tuple-element.9.x_ref, bf16[128,256]{1,0:T(8,128)(2,1)S(1)} %get-tuple-element.10.g_ref, s32[6,2,128]{2,1,0:T(2,128)S(1)} %bitcast.21, s32[6,2,128]{2,1,0:T(2,128)S(1)} %bitcast.23, f32[6,2,128]{2,1,0:T(2,128)S(1)} %bitcast.25, ...), custom_call_target="tpu_custom_call" | custom-call | tf_op jit(solution)/shard_map/expert_exchange/pallas_call | solution.py:358
  40.7 0.0 copy-done.3
  40.7 0.0 copy-done.4
  40.7 22.8 %latent_attention.3 = (bf16[128,256]{1,0:T(8,128)(2,1)S(1)}, bf16[128,256]{1,0:T(8,128)(2,1)S(1)}) custom-call(s32[128]{0:T(128)S(1)} %get-tuple-element.14.order_ref, s32[128]{0:T(128)S(1)} %get-tuple-element.13.slen_ref, s32[1,128]{1,0:T(1,128)S(1)} %bitcast.28, bf16[128,256]{1,0:T(8,128)(2,1)S(1)} %expert_exchange.2.x_in, ...), custom_call_target="tpu_custom_call" | custom-call | tf_op jit(solution)/shard_map/latent_attention/pallas_call | solution.py:216
  63.5 13.4 %expert_exchange.3 = bf16[128,256]{1,0:T(8,128)(2,1)S(1)} custom-call(bf16[128,256]{1,0:T(8,128)(2,1)S(1)} %get-tuple-element.11.x_ref, bf16[128,256]{1,0:T(8,128)(2,1)S(1)} %get-tuple-element.12.g_ref, s32[6,2,128]{2,1,0:T(2,128)S(1)} %bitcast.22, s32[6,2,128]{2,1,0:T(2,128)S(1)} %bitcast.24, f32[6,2,128]{2,1,0:T(2,128)S(1)} %bitcast.26, ...), custom_call_target="tpu_custom_call" | custom-call | tf_op jit(solution)/shard_map/expert_exchange/pallas_call | solution.py:358
  76.9 0.6 copy.16
Async XLA Ops:
  1.6 23.0 %copy-start = (bf16[2,16,256,176]{2,3,1,0:T(8,128)(2,1)S(1)}, bf16[2,16,256,176]{2,3,1,0:T(8,128)(2,1)}, u32[]{:S(2)}) copy-start(bf16[2,16,256,176]{2,3,1,0:T(8,128)(2,1)} %param.22) | copy-start | bytes 8650756
  1.6 23.0 %copy-start.1 = (bf16[2,16,256,176]{2,3,1,0:T(8,128)(2,1)S(1)}, bf16[2,16,256,176]{2,3,1,0:T(8,128)(2,1)}, u32[]{:S(2)}) copy-start(bf16[2,16,256,176]{2,3,1,0:T(8,128)(2,1)} %param.23) | copy-start | bytes 8650756
  1.6 23.0 %copy-start.2 = (bf16[2,16,176,256]{3,2,1,0:T(8,128)(2,1)S(1)}, bf16[2,16,176,256]{3,2,1,0:T(8,128)(2,1)}, u32[]{:S(2)}) copy-start(bf16[2,16,176,256]{3,2,1,0:T(8,128)(2,1)} %w2.3) | copy-start | bytes 8650756
  1.6 23.0 %copy-start.5 = (bf16[2,256,88]{1,2,0:T(8,128)(2,1)S(1)}, bf16[2,256,88]{1,2,0:T(8,128)(2,1)}, u32[]{:S(2)}) copy-start(bf16[2,256,88]{1,2,0:T(8,128)(2,1)} %param.25) | copy-start | bytes 270340
  1.7 23.0 %copy-start.6 = (bf16[2,256,88]{1,2,0:T(8,128)(2,1)S(1)}, bf16[2,256,88]{1,2,0:T(8,128)(2,1)}, u32[]{:S(2)}) copy-start(bf16[2,256,88]{1,2,0:T(8,128)(2,1)} %param.26) | copy-start | bytes 270340
  1.7 23.0 %copy-start.7 = (bf16[2,88,256]{2,1,0:T(8,128)(2,1)S(1)}, bf16[2,88,256]{2,1,0:T(8,128)(2,1)}, u32[]{:S(2)}) copy-start(bf16[2,88,256]{2,1,0:T(8,128)(2,1)} %w2s.3) | copy-start | bytes 270340
  1.7 23.0 %copy-start.8 = (s32[2,128,6]{1,0,2:T(2,128)S(1)}, s32[2,128,6]{1,0,2:T(2,128)}, u32[]{:S(2)}) copy-start(s32[2,128,6]{1,0,2:T(2,128)} %param.19) | copy-start | bytes 18436
  1.7 23.0 %copy-start.9 = (s32[2,128,6]{1,0,2:T(2,128)S(1)}, s32[2,128,6]{1,0,2:T(2,128)}, u32[]{:S(2)}) copy-start(s32[2,128,6]{1,0,2:T(2,128)} %param.20) | copy-start | bytes 18436
  1.7 23.0 %copy-start.10 = (f32[2,128,6]{1,0,2:T(2,128)S(1)}, f32[2,128,6]{1,0,2:T(2,128)}, u32[]{:S(2)}) copy-start(f32[2,128,6]{1,0,2:T(2,128)} %param.21) | copy-start | bytes 18436
  24.7 15.9 %copy-start.3 = (bf16[2,256,1152]{2,1,0:T(8,128)(2,1)S(1)}, bf16[2,256,1152]{2,1,0:T(8,128)(2,1)}, u32[]{:S(2)}) copy-start(bf16[2,256,1152]{2,1,0:T(8,128)(2,1)} %wq_hbm.3) | copy-start | bytes 3538948
  24.8 15.9 %copy-start.4 = (bf16[2,1024,256]{2,1,0:T(8,128)(2,1)S(1)}, bf16[2,1024,256]{2,1,0:T(8,128)(2,1)}, u32[]{:S(2)}) copy-start(bf16[2,1024,256]{2,1,0:T(8,128)(2,1)} %wo_hbm.3) | copy-start | bytes 3145732

commit v5 on v4

--- a/solution.py
+++ b/solution.py
@@ -11,7 +11,7 @@
 LATENT = 512
 CHUNK = 128
 F32 = jnp.float32
-MXU_COLS = 256
+MXU_COLS = (512, 384, 256, 256)
 VBLK = 64
 BF16 = jnp.bfloat16
 
@@ -126,25 +126,28 @@
     def values(g, p):
         slot = lax.rem(g, slots)
         at16 = pl.ds(pl.multiple_of(g * 16, 16), 16)
+        mxu_cols = MXU_COLS[len(p) - 1]
         lhs, rhs = [], []
         for k, t in enumerate(p):
             for j in range(4):
                 for half in range(2):
                     keep = (sub16 == j) & (half16 == half)
                     lhs.append(jnp.where(keep, t, 0.0).astype(BF16))
-                    rhs.append(buf[slot, half, pl.ds(j * kv_dim, MXU_COLS), pl.ds(k * CHUNK, CHUNK)])
+                    rhs.append(buf[slot, half, pl.ds(j * kv_dim, mxu_cols), pl.ds(k * CHUNK, CHUNK)])
         o = lax.dot_general(jnp.concatenate(lhs, axis=1), jnp.concatenate(rhs, axis=1),
                             (((1,), (1,)), ((), ())), preferred_element_type=F32)
-        obuf[at16, :MXU_COLS] = o.astype(BF16)
+        obuf[at16, :mxu_cols] = o.astype(BF16)
+        if mxu_cols == LATENT:
+            return
         rounded = [t.astype(BF16).astype(F32) for t in p]
-        blocks = (LATENT - MXU_COLS) // VBLK
+        blocks = (LATENT - mxu_cols) // VBLK
         picked = [jnp.zeros((VBLK, CHUNK), F32) for _ in range(blocks)]
         for half in range(2):
             for j in range(4):
                 for c in range(blocks):
                     sums = [None, None]
                     for k in range(len(p)):
-                        tile = buf[slot, half, pl.ds(j * kv_dim + MXU_COLS + c * VBLK, VBLK), pl.ds(k * CHUNK, CHUNK)].astype(F32)
+                        tile = buf[slot, half, pl.ds(j * kv_dim + mxu_cols + c * VBLK, VBLK), pl.ds(k * CHUNK, CHUNK)].astype(F32)
                         for head in range(2):
                             row = half * 8 + head * 4 + j
                             term = tile * rounded[k][row:row + 1, :]
@@ -152,7 +155,7 @@
                     for head in range(2):
                         row = half * 8 + head * 4 + j
                         picked[c] = jnp.where(lane_blk == row, jnp.sum(sums[head], axis=1, keepdims=True), picked[c])
-        obuf[at16, MXU_COLS:] = jnp.concatenate(picked, axis=0).T[:16].astype(BF16)
+        obuf[at16, mxu_cols:] = jnp.concatenate(picked, axis=0).T[:16].astype(BF16)
 
     def wait_group(g, nn):
         slot = lax.rem(g, slots)
@@ -315,12 +318,6 @@
         return pltpu.make_async_remote_copy(
             src, dst_ref, psend.at[i], precv.at[i], device_id={'dp': dst}, device_id_type=MESH_ID)
 
-    rcopies[0].wait_recv()
-    gcopies[0].wait_recv()
-    ffn((0, 1))
-    home = send_part(0, acc.at[1], part.at[0], partner)
-    home.start()
-
     rcopies[1].wait_recv()
     gcopies[1].wait_recv()
     ffn((2,))
@@ -339,6 +336,12 @@
         at = pl.ds(i * half, half)
         far.append(send_part(2 + i, acc.at[4, at], part.at[2, at], same))
         far[i].start()
+
+    rcopies[0].wait_recv()
+    gcopies[0].wait_recv()
+    ffn((0, 1))
+    home = send_part(0, acc.at[1], part.at[0], partner)
+    home.start()
     home.wait_recv()
     acc[0] = acc[0] + part[0]
     for i in range(2):

time: 77.6 us -> 74.7 us (0.963)
  Pallas kernels: 75 us -> 71.8 us
    pallas_call x2, Pallas kernels: 45.7 us -> 43.1 us  [attention(): pl.pallas_call(functools.partial(attn_kernel, layer, slots), out_shape=(j...]
where the time goes in v5:
time: 74.7 us; the launch traced here: 74.3 us
  Pallas kernels  71.8 us (96%)
  other arithmetic  1.6 us (2%)
    pallas_call x2, Pallas kernels, attention(): pl.pallas_call(functools.partial(attn_kernel, layer, slots), out_shape=(j...  43.1 us
    pallas_call x2, Pallas kernels, moe(): pl.pallas_call(functools.partial(moe_kernel, layer), out_shape=jax.ShapeD...  28.7 us

profile of v5, /device:TPU:0, one launch (start us, length us, event | category | flops | bytes accessed | tf_op | source)
XLA Modules:
  0.0 74.3 jit_solution(6406210428587466568)
XLA Ops:
  0.0 0.7 and_select_fusion
  0.7 0.2 convert_reduce_fusion
  0.8 0.8 %select_reduce_fusion = (s32[128]{0:T(128)S(1)}, s32[128]{0:T(128)S(1)}) fusion(s32[128]{0:T(128)} %param.15, s32[128]{0:T(128)S(1)} %convert_reduce_fusion), kind=kLoop, calls=%fused_computation | loop fusion | flops 81664 | bytes 2048 | tf_op jit(solution)/shard_map/reduce_sum | solution.py:32
  1.6 0.0 copy-start
  1.6 0.0 copy-start.1
  1.6 0.0 copy-start.2
  1.6 0.0 copy-start.5
  1.7 0.0 copy-start.6
  1.7 0.0 copy-start.7
  1.7 0.0 copy-start.8
  1.7 0.0 copy-start.9
  1.7 0.0 copy-start.10
  1.7 21.6 %latent_attention.2 = (bf16[128,256]{1,0:T(8,128)(2,1)S(1)}, bf16[128,256]{1,0:T(8,128)(2,1)S(1)}) custom-call(s32[128]{0:T(128)S(1)} %get-tuple-element.14.order_ref, s32[128]{0:T(128)S(1)} %get-tuple-element.13.slen_ref, s32[1,128]{1,0:T(1,128)S(1)} %bitcast.27, bf16[128,256]{1,0:T(8,128)(2,1)} %x_in.1, bf16[2,128,576,512]{3,2,1,0:T(8,128)(2,1)} %bitcast.1.cache_ref, ...), custom_call_target="tpu_custom_call" | custom-call | tf_op jit(solution)/shard_map/latent_attention/pallas_call | solution.py:219
  23.4 0.0 copy-done
  23.4 0.0 copy-done.1
  23.4 0.0 copy-done.2
  23.4 0.0 copy-done.5
  23.4 0.0 copy-done.6
  23.4 0.0 copy-done.7
  23.4 0.0 copy-done.8
  23.4 0.0 copy-done.9
  23.4 0.0 copy-done.10
  23.4 0.0 copy-start.3
  23.5 0.0 copy-start.4
  23.5 15.7 %expert_exchange.2.x_in = bf16[128,256]{1,0:T(8,128)(2,1)S(1)} custom-call(bf16[128,256]{1,0:T(8,128)(2,1)S(1)} %get-tuple-element.9.x_ref, bf16[128,256]{1,0:T(8,128)(2,1)S(1)} %get-tuple-element.10.g_ref, s32[6,2,128]{2,1,0:T(2,128)S(1)} %bitcast.21, s32[6,2,128]{2,1,0:T(2,128)S(1)} %bitcast.23, f32[6,2,128]{2,1,0:T(2,128)S(1)} %bitcast.25, ...), custom_call_target="tpu_custom_call" | custom-call | tf_op jit(solution)/shard_map/expert_exchange/pallas_call | solution.py:361
  39.2 0.0 copy-done.3
  39.2 0.0 copy-done.4
  39.2 21.5 %latent_attention.3 = (bf16[128,256]{1,0:T(8,128)(2,1)S(1)}, bf16[128,256]{1,0:T(8,128)(2,1)S(1)}) custom-call(s32[128]{0:T(128)S(1)} %get-tuple-element.14.order_ref, s32[128]{0:T(128)S(1)} %get-tuple-element.13.slen_ref, s32[1,128]{1,0:T(1,128)S(1)} %bitcast.28, bf16[128,256]{1,0:T(8,128)(2,1)S(1)} %expert_exchange.2.x_in, ...), custom_call_target="tpu_custom_call" | custom-call | tf_op jit(solution)/shard_map/latent_attention/pallas_call | solution.py:219
  60.6 13.0 %expert_exchange.3 = bf16[128,256]{1,0:T(8,128)(2,1)S(1)} custom-call(bf16[128,256]{1,0:T(8,128)(2,1)S(1)} %get-tuple-element.11.x_ref, bf16[128,256]{1,0:T(8,128)(2,1)S(1)} %get-tuple-element.12.g_ref, s32[6,2,128]{2,1,0:T(2,128)S(1)} %bitcast.22, s32[6,2,128]{2,1,0:T(2,128)S(1)} %bitcast.24, f32[6,2,128]{2,1,0:T(2,128)S(1)} %bitcast.26, ...), custom_call_target="tpu_custom_call" | custom-call | tf_op jit(solution)/shard_map/expert_exchange/pallas_call | solution.py:361
  73.7 0.6 copy.16
Async XLA Ops:
  1.6 21.7 %copy-start = (bf16[2,16,256,176]{2,3,1,0:T(8,128)(2,1)S(1)}, bf16[2,16,256,176]{2,3,1,0:T(8,128)(2,1)}, u32[]{:S(2)}) copy-start(bf16[2,16,256,176]{2,3,1,0:T(8,128)(2,1)} %param.22) | copy-start | bytes 8650756
  1.6 21.7 %copy-start.1 = (bf16[2,16,256,176]{2,3,1,0:T(8,128)(2,1)S(1)}, bf16[2,16,256,176]{2,3,1,0:T(8,128)(2,1)}, u32[]{:S(2)}) copy-start(bf16[2,16,256,176]{2,3,1,0:T(8,128)(2,1)} %param.23) | copy-start | bytes 8650756
  1.6 21.7 %copy-start.2 = (bf16[2,16,176,256]{3,2,1,0:T(8,128)(2,1)S(1)}, bf16[2,16,176,256]{3,2,1,0:T(8,128)(2,1)}, u32[]{:S(2)}) copy-start(bf16[2,16,176,256]{3,2,1,0:T(8,128)(2,1)} %w2.3) | copy-start | bytes 8650756
  1.6 21.7 %copy-start.5 = (bf16[2,256,88]{1,2,0:T(8,128)(2,1)S(1)}, bf16[2,256,88]{1,2,0:T(8,128)(2,1)}, u32[]{:S(2)}) copy-start(bf16[2,256,88]{1,2,0:T(8,128)(2,1)} %param.25) | copy-start | bytes 270340
  1.7 21.7 %copy-start.6 = (bf16[2,256,88]{1,2,0:T(8,128)(2,1)S(1)}, bf16[2,256,88]{1,2,0:T(8,128)(2,1)}, u32[]{:S(2)}) copy-start(bf16[2,256,88]{1,2,0:T(8,128)(2,1)} %param.26) | copy-start | bytes 270340
  1.7 21.7 %copy-start.7 = (bf16[2,88,256]{2,1,0:T(8,128)(2,1)S(1)}, bf16[2,88,256]{2,1,0:T(8,128)(2,1)}, u32[]{:S(2)}) copy-start(bf16[2,88,256]{2,1,0:T(8,128)(2,1)} %w2s.3) | copy-start | bytes 270340
  1.7 21.7 %copy-start.8 = (s32[2,128,6]{1,0,2:T(2,128)S(1)}, s32[2,128,6]{1,0,2:T(2,128)}, u32[]{:S(2)}) copy-start(s32[2,128,6]{1,0,2:T(2,128)} %param.19) | copy-start | bytes 18436
  1.7 21.7 %copy-start.9 = (s32[2,128,6]{1,0,2:T(2,128)S(1)}, s32[2,128,6]{1,0,2:T(2,128)}, u32[]{:S(2)}) copy-start(s32[2,128,6]{1,0,2:T(2,128)} %param.20) | copy-start | bytes 18436
  1.7 21.7 %copy-start.10 = (f32[2,128,6]{1,0,2:T(2,128)S(1)}, f32[2,128,6]{1,0,2:T(2,128)}, u32[]{:S(2)}) copy-start(f32[2,128,6]{1,0,2:T(2,128)} %param.21) | copy-start | bytes 18436
  23.4 15.7 %copy-start.3 = (bf16[2,256,1152]{2,1,0:T(8,128)(2,1)S(1)}, bf16[2,256,1152]{2,1,0:T(8,128)(2,1)}, u32[]{:S(2)}) copy-start(bf16[2,256,1152]{2,1,0:T(8,128)(2,1)} %wq_hbm.3) | copy-start | bytes 3538948
  23.5 15.7 %copy-start.4 = (bf16[2,1024,256]{2,1,0:T(8,128)(2,1)S(1)}, bf16[2,1024,256]{2,1,0:T(8,128)(2,1)}, u32[]{:S(2)}) copy-start(bf16[2,1024,256]{2,1,0:T(8,128)(2,1)} %wo_hbm.3) | copy-start | bytes 3145732

commit v6 on v5

--- a/solution.py
+++ b/solution.py
@@ -238,7 +238,7 @@
 
 
 MESH_ID = pl.DeviceIdType.MESH
-EXP_STEP = 4
+EXP_STEP = 8
 
 
 def moe_kernel(layer, x_ref, g_ref, ids_ref, slot_ref, gate_ref, w1, w3, w2, w1s, w3s, w2s, out_ref,
@@ -253,16 +253,15 @@
     _, experts, ff, d_model = w2.shape
     toks = x_ref.shape[0]
 
+    barrier = pltpu.get_barrier_semaphore()
+    for p in peers:
+        pl.semaphore_signal(barrier, inc=1, device_id={'dp': p}, device_id_type=MESH_ID)
     expert_id = lax.broadcasted_iota(jnp.int32, route_ref.shape, 0)
     route = jnp.zeros(route_ref.shape, F32)
     for j in range(ids_ref.shape[0]):
         hit = (ids_ref[j, layer:layer + 1, :] == expert_id) & (slot_ref[j, layer:layer + 1, :] >= 0)
         route = route + jnp.where(hit, gate_ref[j, layer:layer + 1, :], 0.0)
     route_ref[...] = route
-
-    barrier = pltpu.get_barrier_semaphore()
-    for p in peers:
-        pl.semaphore_signal(barrier, inc=1, device_id={'dp': p}, device_id_type=MESH_ID)
     pl.semaphore_wait(barrier, 3)
 
     gcopies, rcopies = [], []

time: 74.7 us -> 74.1 us (level)
  no operation moved by 1% of the time
where the time goes in v6:
time: 74.1 us; the launch traced here: 74.3 us
  Pallas kernels  71.8 us (97%)
  other arithmetic  1.6 us (2%)
    pallas_call x2, Pallas kernels, attention(): pl.pallas_call(functools.partial(attn_kernel, layer, slots), out_shape=(j...  43.1 us
    pallas_call x2, Pallas kernels, moe(): pl.pallas_call(functools.partial(moe_kernel, layer), out_shape=jax.ShapeD...  28.7 us

profile of v6, /device:TPU:0, one launch (start us, length us, event | category | flops | bytes accessed | tf_op | source)
XLA Modules:
  0.0 74.3 jit_solution(1626112991126905387)
XLA Ops:
  0.0 0.7 and_select_fusion
  0.7 0.2 convert_reduce_fusion
  0.8 0.8 %select_reduce_fusion = (s32[128]{0:T(128)S(1)}, s32[128]{0:T(128)S(1)}) fusion(s32[128]{0:T(128)} %param.15, s32[128]{0:T(128)S(1)} %convert_reduce_fusion), kind=kLoop, calls=%fused_computation | loop fusion | flops 81664 | bytes 2048 | tf_op jit(solution)/shard_map/reduce_sum | solution.py:32
  1.6 0.0 copy-start
  1.6 0.0 copy-start.1
  1.6 0.0 copy-start.2
  1.6 0.0 copy-start.5
  1.7 0.0 copy-start.6
  1.7 0.0 copy-start.7
  1.7 0.0 copy-start.8
  1.7 0.0 copy-start.9
  1.7 0.0 copy-start.10
  1.7 21.6 %latent_attention.2 = (bf16[128,256]{1,0:T(8,128)(2,1)S(1)}, bf16[128,256]{1,0:T(8,128)(2,1)S(1)}) custom-call(s32[128]{0:T(128)S(1)} %get-tuple-element.14.order_ref, s32[128]{0:T(128)S(1)} %get-tuple-element.13.slen_ref, s32[1,128]{1,0:T(1,128)S(1)} %bitcast.27, bf16[128,256]{1,0:T(8,128)(2,1)} %x_in.1, bf16[2,128,576,512]{3,2,1,0:T(8,128)(2,1)} %bitcast.1.cache_ref, ...), custom_call_target="tpu_custom_call" | custom-call | tf_op jit(solution)/shard_map/latent_attention/pallas_call | solution.py:219
  23.4 0.0 copy-done
  23.4 0.0 copy-done.1
  23.4 0.0 copy-done.2
  23.4 0.0 copy-done.5
  23.4 0.0 copy-done.6
  23.4 0.0 copy-done.7
  23.4 0.0 copy-done.8
  23.4 0.0 copy-done.9
  23.4 0.0 copy-done.10
  23.4 0.0 copy-start.3
  23.5 0.0 copy-start.4
  23.5 16.0 %expert_exchange.2.x_in = bf16[128,256]{1,0:T(8,128)(2,1)S(1)} custom-call(bf16[128,256]{1,0:T(8,128)(2,1)S(1)} %get-tuple-element.9.x_ref, bf16[128,256]{1,0:T(8,128)(2,1)S(1)} %get-tuple-element.10.g_ref, s32[6,2,128]{2,1,0:T(2,128)S(1)} %bitcast.21, s32[6,2,128]{2,1,0:T(2,128)S(1)} %bitcast.23, f32[6,2,128]{2,1,0:T(2,128)S(1)} %bitcast.25, ...), custom_call_target="tpu_custom_call" | custom-call | tf_op jit(solution)/shard_map/expert_exchange/pallas_call | solution.py:360
  39.5 0.0 copy-done.3
  39.5 0.0 copy-done.4
  39.5 21.5 %latent_attention.3 = (bf16[128,256]{1,0:T(8,128)(2,1)S(1)}, bf16[128,256]{1,0:T(8,128)(2,1)S(1)}) custom-call(s32[128]{0:T(128)S(1)} %get-tuple-element.14.order_ref, s32[128]{0:T(128)S(1)} %get-tuple-element.13.slen_ref, s32[1,128]{1,0:T(1,128)S(1)} %bitcast.28, bf16[128,256]{1,0:T(8,128)(2,1)S(1)} %expert_exchange.2.x_in, ...), custom_call_target="tpu_custom_call" | custom-call | tf_op jit(solution)/shard_map/latent_attention/pallas_call | solution.py:219
  61.0 12.7 %expert_exchange.3 = bf16[128,256]{1,0:T(8,128)(2,1)S(1)} custom-call(bf16[128,256]{1,0:T(8,128)(2,1)S(1)} %get-tuple-element.11.x_ref, bf16[128,256]{1,0:T(8,128)(2,1)S(1)} %get-tuple-element.12.g_ref, s32[6,2,128]{2,1,0:T(2,128)S(1)} %bitcast.22, s32[6,2,128]{2,1,0:T(2,128)S(1)} %bitcast.24, f32[6,2,128]{2,1,0:T(2,128)S(1)} %bitcast.26, ...), custom_call_target="tpu_custom_call" | custom-call | tf_op jit(solution)/shard_map/expert_exchange/pallas_call | solution.py:360
  73.7 0.6 copy.16
Async XLA Ops:
  1.6 21.7 %copy-start = (bf16[2,16,256,176]{2,3,1,0:T(8,128)(2,1)S(1)}, bf16[2,16,256,176]{2,3,1,0:T(8,128)(2,1)}, u32[]{:S(2)}) copy-start(bf16[2,16,256,176]{2,3,1,0:T(8,128)(2,1)} %param.22) | copy-start | bytes 8650756
  1.6 21.7 %copy-start.1 = (bf16[2,16,256,176]{2,3,1,0:T(8,128)(2,1)S(1)}, bf16[2,16,256,176]{2,3,1,0:T(8,128)(2,1)}, u32[]{:S(2)}) copy-start(bf16[2,16,256,176]{2,3,1,0:T(8,128)(2,1)} %param.23) | copy-start | bytes 8650756
  1.6 21.7 %copy-start.2 = (bf16[2,16,176,256]{3,2,1,0:T(8,128)(2,1)S(1)}, bf16[2,16,176,256]{3,2,1,0:T(8,128)(2,1)}, u32[]{:S(2)}) copy-start(bf16[2,16,176,256]{3,2,1,0:T(8,128)(2,1)} %w2.3) | copy-start | bytes 8650756
  1.6 21.7 %copy-start.5 = (bf16[2,256,88]{1,2,0:T(8,128)(2,1)S(1)}, bf16[2,256,88]{1,2,0:T(8,128)(2,1)}, u32[]{:S(2)}) copy-start(bf16[2,256,88]{1,2,0:T(8,128)(2,1)} %param.25) | copy-start | bytes 270340
  1.7 21.7 %copy-start.6 = (bf16[2,256,88]{1,2,0:T(8,128)(2,1)S(1)}, bf16[2,256,88]{1,2,0:T(8,128)(2,1)}, u32[]{:S(2)}) copy-start(bf16[2,256,88]{1,2,0:T(8,128)(2,1)} %param.26) | copy-start | bytes 270340
  1.7 21.7 %copy-start.7 = (bf16[2,88,256]{2,1,0:T(8,128)(2,1)S(1)}, bf16[2,88,256]{2,1,0:T(8,128)(2,1)}, u32[]{:S(2)}) copy-start(bf16[2,88,256]{2,1,0:T(8,128)(2,1)} %w2s.3) | copy-start | bytes 270340
  1.7 21.7 %copy-start.8 = (s32[2,128,6]{1,0,2:T(2,128)S(1)}, s32[2,128,6]{1,0,2:T(2,128)}, u32[]{:S(2)}) copy-start(s32[2,128,6]{1,0,2:T(2,128)} %param.19) | copy-start | bytes 18436
  1.7 21.7 %copy-start.9 = (s32[2,128,6]{1,0,2:T(2,128)S(1)}, s32[2,128,6]{1,0,2:T(2,128)}, u32[]{:S(2)}) copy-start(s32[2,128,6]{1,0,2:T(2,128)} %param.20) | copy-start | bytes 18436
  1.7 21.7 %copy-start.10 = (f32[2,128,6]{1,0,2:T(2,128)S(1)}, f32[2,128,6]{1,0,2:T(2,128)}, u32[]{:S(2)}) copy-start(f32[2,128,6]{1,0,2:T(2,128)} %param.21) | copy-start | bytes 18436
  23.4 16.0 %copy-start.3 = (bf16[2,256,1152]{2,1,0:T(8,128)(2,1)S(1)}, bf16[2,256,1152]{2,1,0:T(8,128)(2,1)}, u32[]{:S(2)}) copy-start(bf16[2,256,1152]{2,1,0:T(8,128)(2,1)} %wq_hbm.3) | copy-start | bytes 3538948
  23.5 16.0 %copy-start.4 = (bf16[2,1024,256]{2,1,0:T(8,128)(2,1)S(1)}, bf16[2,1024,256]{2,1,0:T(8,128)(2,1)}, u32[]{:S(2)}) copy-start(bf16[2,1024,256]{2,1,0:T(8,128)(2,1)} %wo_hbm.3) | copy-start | bytes 3145732
